TPU v7x, 32 devices: a whole 2x2x4 slice. The times are simulated.
32 devices in a mesh: ang: 8 (over y, x, core), img: 4 (over z).
Axes of the slice: x: 2, y: 2, z: 4, core: 2. Of those that a mesh axis runs over, the one named last changes fastest.
Arguments:
- sinogram: bfloat16 [16, 64, 4096], P('ang', None, 'img'), may hold values from -4 to 28
- offsets: int32 [16], replicated, may hold values from 0 to 65504, as said below
- steps: int32 [16, 2], replicated, may hold values from -32 to 32, as said below
Outputs:
- picture: bfloat16 [1024, 64, 1024], P('ang', None, 'img')
Inputs may be any that keep to these rules, and one draw needn't show every extreme that they name: Each row (u, v) of steps satisfies u^2 + v^2 <= 32^2 < (|u| + 1)^2 + (|v| + 1)^2. For every angle a and every pixel (y, x) with 0 <= x, y < 1024, offsets[a] + steps[a, 0] x + steps[a, 1] y lies in 0 to 65504.
All inputs are finite; a program needn't handle non-finite values.
Results may differ from a plain program's by a relative error of at most 0.0053.
Values may be sent and summed in bfloat16 or wider, within the bound.
No kernel may reach another device: no remote copies, remote signals or barrier semaphores. Data moves between devices by JAX's collectives and lax.ppermute only.
A program may use at most 192 MiB of HBM per device.

v0:
```python
import math

import jax
import jax.numpy as jnp
from jax import lax
from jax.sharding import PartitionSpec as P

BINS = 4096
IMG = 1024
TILE = 32
BAND = 128


def ramp_table():
    bin_index = jnp.arange(BINS, dtype=jnp.int32)
    offset_gap = bin_index[None, :] - bin_index[:, None]
    safe_gap = jnp.where(offset_gap == 0, 1, offset_gap).astype(jnp.float32)
    odd_gap = offset_gap % 2 != 0
    kernel = jnp.where(
        offset_gap == 0,
        jnp.float32(0.25),
        jnp.where(odd_gap, -1.0 / (math.pi**2 * safe_gap * safe_gap), jnp.float32(0.0)),
    )
    return kernel


def project_block(filtered, geo_offsets, geo_steps, row_top, row_count, col_left, col_count):
    slices = filtered.shape[1]
    across = col_count // TILE
    block_rows = min(row_count, 8 * TILE)
    while row_count % block_rows:
        block_rows = block_rows - TILE
    tiles_down = block_rows // TILE
    tile_count = tiles_down * across
    tile_order = jnp.arange(tile_count, dtype=jnp.int32)
    tile_top = tile_order // across * TILE
    tile_left = tile_order % across * TILE + col_left
    in_tile = jnp.arange(TILE * TILE, dtype=jnp.int32)
    pix_row = in_tile // TILE
    pix_col = in_tile % TILE
    band_slot = jnp.arange(BAND, dtype=jnp.int32)[None, :, None]

    def one_block(block_no):
        block_top = row_top + block_no * block_rows

        def one_angle(summed, angle_data):
            filtered_one, offset, step_pair = angle_data
            step_x = step_pair[0]
            step_y = step_pair[1]
            corner = offset + step_x * tile_left + step_y * (block_top + tile_top)
            corner = (
                corner + jnp.minimum(step_x, 0) * (TILE - 1) + jnp.minimum(step_y, 0) * (TILE - 1)
            )
            band_start = jnp.minimum(corner // 16, BINS - BAND)
            band_rows = jax.vmap(
                lambda begin_at: lax.dynamic_slice_in_dim(filtered_one, begin_at, BAND, 1)
            )(band_start)
            position = (
                offset
                + step_x * (tile_left[:, None] + pix_col[None, :])
                + step_y * (block_top + tile_top[:, None] + pix_row[None, :])
            )
            low_bin = (position // 16 - band_start[:, None])[:, None, :]
            upper_weight = ((position % 16).astype(jnp.float32) / 16.0)[:, None, :]
            weights = jnp.where(band_slot == low_bin, 1.0 - upper_weight, 0.0) + jnp.where(
                band_slot == low_bin + 1, upper_weight, 0.0
            )
            weights = weights.astype(jnp.bfloat16)
            contrib = jnp.einsum(
                "tsb,tbp->tsp", band_rows, weights, preferred_element_type=jnp.float32
            )
            return (summed + contrib, None)

        start_sum = jnp.zeros((tile_count, slices, TILE * TILE), jnp.float32)
        summed = lax.scan(one_angle, start_sum, (filtered, geo_offsets, geo_steps))[0]
        summed = summed.reshape(tiles_down, across, slices, TILE, TILE)
        return jnp.transpose(summed, (0, 3, 2, 1, 4)).reshape(block_rows, slices, col_count)

    blocks = lax.map(one_block, jnp.arange(row_count // block_rows, dtype=jnp.int32))
    return blocks.reshape(row_count, slices, col_count)


def shards(sinogram, offsets, steps):
    angles_dev = sinogram.shape[0]
    ramp_rows = ramp_table()
    whole_bins = lax.all_gather(sinogram, "img", axis=2, tiled=True)
    result = jnp.dot(
        whole_bins.reshape(-1, BINS).astype(jnp.float32),
        ramp_rows,
        precision=lax.Precision.HIGHEST,
        preferred_element_type=jnp.float32,
    )
    filtered = result.astype(jnp.bfloat16).reshape(whole_bins.shape[0], whole_bins.shape[1], BINS)
    ang_count = lax.axis_size("ang")
    img_count = lax.axis_size("img")
    rows_dev = IMG // ang_count
    cols_dev = IMG // img_count
    col_left = lax.axis_index("img") * cols_dev
    total_angles = angles_dev * ang_count
    row_first = lax.axis_index("ang") * rows_dev
    partial_value = project_block(
        lax.all_gather(filtered, "ang", axis=0, tiled=True),
        offsets,
        steps,
        row_first,
        rows_dev,
        col_left,
        cols_dev,
    )
    return (partial_value * (2.0 / math.sqrt(total_angles))).astype(jnp.bfloat16)


def solution(mesh):
    return jax.shard_map(
        shards,
        mesh=mesh,
        in_specs=(P("ang", None, "img"), P(), P()),
        out_specs=P("ang", None, "img"),
        check_vma=False,
    )
```

profile of v0, /device:TPU:0, one launch (start us, length us, event | category | flops | bytes accessed | tf_op | source)
XLA Modules:
  0.0 1140.7 jit_solution(4788914753813361589)
XLA Ops:
  7.3 32.3 %all-gather.3.cloned.1.call-done = bf16[2,64,4096]{2,1,0:T(8,128)(2,1)} async-done(((bf16[2,64,1024]{2,1,0:T(8,128)(2,1)}), bf16[2,64,4096]{2,1,0:T(8,128)(2,1)}) %all-gather.3.cloned.1.call-update) | async-done | bytes 1048592 | tf_op jit(solution)/shard_map/all_gather | solution.py:86
  39.6 77.5 %fusion.51 = bf16[4096,128]{0,1:T(8,128)(2,1)} fusion(bf16[128,4096]{1,0:T(8,128)(2,1)} %bitcast.47), kind=kOutput, calls=%fused_computation.90 | convolution fusion | flops 26122649600 | bytes 2097152 | tf_op jit(solution)/shard_map/dot_general | solution.py:87
  117.1 53.8 %all-gather.5.cloned.1.call-done = bf16[16,64,4096]{2,1,0:T(8,128)(2,1)} async-done(((bf16[2,64,4096]{2,1,0:T(8,128)(2,1)}), bf16[16,64,4096]{2,1,0:T(8,128)(2,1)}) %all-gather.5.cloned.1.call-update) | async-done | bytes 8388624 | tf_op jit(solution)/shard_map/all_gather | solution.py:102
  170.9 923.8 %while.27 = (s32[]{:T(128)}, f32[32,64,1024]{2,1,0:T(8,128)}, bf16[16,64,4096]{2,1,0:T(8,128)(2,1)}, s32[16]{0:T(128)S(1)}, s32[16,2]{0,1:T(2,128)S(1)}, /*index...) while((s32[]{:T(128)}, f32[32,64,1024]{2,1,0:T(8,128)}, ...), condition=%wide.region_1.2_spmd.clone.clone, body=%wide.region_0.1_spmd.clone.clone.sunk | while | flops 567654720 | bytes 19458236 | solution.py:75
  180.3 39.0 %while.28 = (s32[]{:T(128)}, bf16[64,4096]{1,0:T(8,128)(2,1)S(1)}, s32[32,2]{0,1:T(2,128)S(1)}, bf16[32,64,128]{2,1,0:T(8,128)(2,1)S(1)}, s32[]{:T(128)}) while((s32[]{:T(128)}, bf16[64,4096]{1,0:T(8,128)(2,1)S(1)}, s32[32,2]{0,1:T(2,128)S(1)}, bf16[32,64,128]{2,1,0:T(8,128)(2,1)S(1)}, s32[]{:T(128)}) %tuple.73), condition=%wide.while_cond, body=%wide.while_body.sunk | while | flops 2 | bytes 32873 | solution.py:56
  236.0 39.0 %while.28 = (s32[]{:T(128)}, bf16[64,4096]{1,0:T(8,128)(2,1)S(1)}, s32[32,2]{0,1:T(2,128)S(1)}, bf16[32,64,128]{2,1,0:T(8,128)(2,1)S(1)}, s32[]{:T(128)}) while((s32[]{:T(128)}, bf16[64,4096]{1,0:T(8,128)(2,1)S(1)}, s32[32,2]{0,1:T(2,128)S(1)}, bf16[32,64,128]{2,1,0:T(8,128)(2,1)S(1)}, s32[]{:T(128)}) %tuple.73), condition=%wide.while_cond, body=%wide.while_body.sunk | while | flops 2 | bytes 32873 | solution.py:56
  293.9 39.0 %while.28 = (s32[]{:T(128)}, bf16[64,4096]{1,0:T(8,128)(2,1)S(1)}, s32[32,2]{0,1:T(2,128)S(1)}, bf16[32,64,128]{2,1,0:T(8,128)(2,1)S(1)}, s32[]{:T(128)}) while((s32[]{:T(128)}, bf16[64,4096]{1,0:T(8,128)(2,1)S(1)}, s32[32,2]{0,1:T(2,128)S(1)}, bf16[32,64,128]{2,1,0:T(8,128)(2,1)S(1)}, s32[]{:T(128)}) %tuple.73), condition=%wide.while_cond, body=%wide.while_body.sunk | while | flops 2 | bytes 32873 | solution.py:56
  351.8 39.0 %while.28 = (s32[]{:T(128)}, bf16[64,4096]{1,0:T(8,128)(2,1)S(1)}, s32[32,2]{0,1:T(2,128)S(1)}, bf16[32,64,128]{2,1,0:T(8,128)(2,1)S(1)}, s32[]{:T(128)}) while((s32[]{:T(128)}, bf16[64,4096]{1,0:T(8,128)(2,1)S(1)}, s32[32,2]{0,1:T(2,128)S(1)}, bf16[32,64,128]{2,1,0:T(8,128)(2,1)S(1)}, s32[]{:T(128)}) %tuple.73), condition=%wide.while_cond, body=%wide.while_body.sunk | while | flops 2 | bytes 32873 | solution.py:56
  409.6 39.0 %while.28 = (s32[]{:T(128)}, bf16[64,4096]{1,0:T(8,128)(2,1)S(1)}, s32[32,2]{0,1:T(2,128)S(1)}, bf16[32,64,128]{2,1,0:T(8,128)(2,1)S(1)}, s32[]{:T(128)}) while((s32[]{:T(128)}, bf16[64,4096]{1,0:T(8,128)(2,1)S(1)}, s32[32,2]{0,1:T(2,128)S(1)}, bf16[32,64,128]{2,1,0:T(8,128)(2,1)S(1)}, s32[]{:T(128)}) %tuple.73), condition=%wide.while_cond, body=%wide.while_body.sunk | while | flops 2 | bytes 32873 | solution.py:56
  467.5 39.0 %while.28 = (s32[]{:T(128)}, bf16[64,4096]{1,0:T(8,128)(2,1)S(1)}, s32[32,2]{0,1:T(2,128)S(1)}, bf16[32,64,128]{2,1,0:T(8,128)(2,1)S(1)}, s32[]{:T(128)}) while((s32[]{:T(128)}, bf16[64,4096]{1,0:T(8,128)(2,1)S(1)}, s32[32,2]{0,1:T(2,128)S(1)}, bf16[32,64,128]{2,1,0:T(8,128)(2,1)S(1)}, s32[]{:T(128)}) %tuple.73), condition=%wide.while_cond, body=%wide.while_body.sunk | while | flops 2 | bytes 32873 | solution.py:56
  506.5 9.5 select_add_fusion.2
  525.4 39.0 %while.28 = (s32[]{:T(128)}, bf16[64,4096]{1,0:T(8,128)(2,1)S(1)}, s32[32,2]{0,1:T(2,128)S(1)}, bf16[32,64,128]{2,1,0:T(8,128)(2,1)S(1)}, s32[]{:T(128)}) while((s32[]{:T(128)}, bf16[64,4096]{1,0:T(8,128)(2,1)S(1)}, s32[32,2]{0,1:T(2,128)S(1)}, bf16[32,64,128]{2,1,0:T(8,128)(2,1)S(1)}, s32[]{:T(128)}) %tuple.73), condition=%wide.while_cond, body=%wide.while_body.sunk | while | flops 2 | bytes 32873 | solution.py:56
  583.3 39.0 %while.28 = (s32[]{:T(128)}, bf16[64,4096]{1,0:T(8,128)(2,1)S(1)}, s32[32,2]{0,1:T(2,128)S(1)}, bf16[32,64,128]{2,1,0:T(8,128)(2,1)S(1)}, s32[]{:T(128)}) while((s32[]{:T(128)}, bf16[64,4096]{1,0:T(8,128)(2,1)S(1)}, s32[32,2]{0,1:T(2,128)S(1)}, bf16[32,64,128]{2,1,0:T(8,128)(2,1)S(1)}, s32[]{:T(128)}) %tuple.73), condition=%wide.while_cond, body=%wide.while_body.sunk | while | flops 2 | bytes 32873 | solution.py:56
  641.1 39.0 %while.28 = (s32[]{:T(128)}, bf16[64,4096]{1,0:T(8,128)(2,1)S(1)}, s32[32,2]{0,1:T(2,128)S(1)}, bf16[32,64,128]{2,1,0:T(8,128)(2,1)S(1)}, s32[]{:T(128)}) while((s32[]{:T(128)}, bf16[64,4096]{1,0:T(8,128)(2,1)S(1)}, s32[32,2]{0,1:T(2,128)S(1)}, bf16[32,64,128]{2,1,0:T(8,128)(2,1)S(1)}, s32[]{:T(128)}) %tuple.73), condition=%wide.while_cond, body=%wide.while_body.sunk | while | flops 2 | bytes 32873 | solution.py:56
  680.2 9.5 select_add_fusion.2
  699.0 39.0 %while.28 = (s32[]{:T(128)}, bf16[64,4096]{1,0:T(8,128)(2,1)S(1)}, s32[32,2]{0,1:T(2,128)S(1)}, bf16[32,64,128]{2,1,0:T(8,128)(2,1)S(1)}, s32[]{:T(128)}) while((s32[]{:T(128)}, bf16[64,4096]{1,0:T(8,128)(2,1)S(1)}, s32[32,2]{0,1:T(2,128)S(1)}, bf16[32,64,128]{2,1,0:T(8,128)(2,1)S(1)}, s32[]{:T(128)}) %tuple.73), condition=%wide.while_cond, body=%wide.while_body.sunk | while | flops 2 | bytes 32873 | solution.py:56
  756.9 39.0 %while.28 = (s32[]{:T(128)}, bf16[64,4096]{1,0:T(8,128)(2,1)S(1)}, s32[32,2]{0,1:T(2,128)S(1)}, bf16[32,64,128]{2,1,0:T(8,128)(2,1)S(1)}, s32[]{:T(128)}) while((s32[]{:T(128)}, bf16[64,4096]{1,0:T(8,128)(2,1)S(1)}, s32[32,2]{0,1:T(2,128)S(1)}, bf16[32,64,128]{2,1,0:T(8,128)(2,1)S(1)}, s32[]{:T(128)}) %tuple.73), condition=%wide.while_cond, body=%wide.while_body.sunk | while | flops 2 | bytes 32873 | solution.py:56
  814.8 39.0 %while.28 = (s32[]{:T(128)}, bf16[64,4096]{1,0:T(8,128)(2,1)S(1)}, s32[32,2]{0,1:T(2,128)S(1)}, bf16[32,64,128]{2,1,0:T(8,128)(2,1)S(1)}, s32[]{:T(128)}) while((s32[]{:T(128)}, bf16[64,4096]{1,0:T(8,128)(2,1)S(1)}, s32[32,2]{0,1:T(2,128)S(1)}, bf16[32,64,128]{2,1,0:T(8,128)(2,1)S(1)}, s32[]{:T(128)}) %tuple.73), condition=%wide.while_cond, body=%wide.while_body.sunk | while | flops 2 | bytes 32873 | solution.py:56
  853.8 9.5 select_add_fusion.2
  872.6 39.0 %while.28 = (s32[]{:T(128)}, bf16[64,4096]{1,0:T(8,128)(2,1)S(1)}, s32[32,2]{0,1:T(2,128)S(1)}, bf16[32,64,128]{2,1,0:T(8,128)(2,1)S(1)}, s32[]{:T(128)}) while((s32[]{:T(128)}, bf16[64,4096]{1,0:T(8,128)(2,1)S(1)}, s32[32,2]{0,1:T(2,128)S(1)}, bf16[32,64,128]{2,1,0:T(8,128)(2,1)S(1)}, s32[]{:T(128)}) %tuple.73), condition=%wide.while_cond, body=%wide.while_body.sunk | while | flops 2 | bytes 32873 | solution.py:56
  930.5 39.0 %while.28 = (s32[]{:T(128)}, bf16[64,4096]{1,0:T(8,128)(2,1)S(1)}, s32[32,2]{0,1:T(2,128)S(1)}, bf16[32,64,128]{2,1,0:T(8,128)(2,1)S(1)}, s32[]{:T(128)}) while((s32[]{:T(128)}, bf16[64,4096]{1,0:T(8,128)(2,1)S(1)}, s32[32,2]{0,1:T(2,128)S(1)}, bf16[32,64,128]{2,1,0:T(8,128)(2,1)S(1)}, s32[]{:T(128)}) %tuple.73), condition=%wide.while_cond, body=%wide.while_body.sunk | while | flops 2 | bytes 32873 | solution.py:56
  988.4 39.0 %while.28 = (s32[]{:T(128)}, bf16[64,4096]{1,0:T(8,128)(2,1)S(1)}, s32[32,2]{0,1:T(2,128)S(1)}, bf16[32,64,128]{2,1,0:T(8,128)(2,1)S(1)}, s32[]{:T(128)}) while((s32[]{:T(128)}, bf16[64,4096]{1,0:T(8,128)(2,1)S(1)}, s32[32,2]{0,1:T(2,128)S(1)}, bf16[32,64,128]{2,1,0:T(8,128)(2,1)S(1)}, s32[]{:T(128)}) %tuple.73), condition=%wide.while_cond, body=%wide.while_body.sunk | while | flops 2 | bytes 32873 | solution.py:56
  1046.3 39.0 %while.28 = (s32[]{:T(128)}, bf16[64,4096]{1,0:T(8,128)(2,1)S(1)}, s32[32,2]{0,1:T(2,128)S(1)}, bf16[32,64,128]{2,1,0:T(8,128)(2,1)S(1)}, s32[]{:T(128)}) while((s32[]{:T(128)}, bf16[64,4096]{1,0:T(8,128)(2,1)S(1)}, s32[32,2]{0,1:T(2,128)S(1)}, bf16[32,64,128]{2,1,0:T(8,128)(2,1)S(1)}, s32[]{:T(128)}) %tuple.73), condition=%wide.while_cond, body=%wide.while_body.sunk | while | flops 2 | bytes 32873 | solution.py:56
  1094.8 12.2 %copy.8 = f32[32,64,1024]{1,2,0:T(8,128)} copy(f32[32,64,1024]{2,1,0:T(8,128)} %get-tuple-element.215) | data formatting | bytes 16777216 | tf_op jit(solution)/shard_map/while/body/eval_jaxpr/while | solution.py:75
  (1753 shorter events, 895.0 us)
Async XLA Ops:
  6.5 33.1 %all-gather.3.cloned.1.call-start = ((), (), s32[]{:S(2)}) async-start(), calls=%async_computation | async-start | bytes 1310720 | tf_op jit(solution)/shard_map/all_gather | solution.py:86
  7.3 163.7 %all-gather.5.cloned.1.call-start = ((), (), s32[]{:S(2)}) async-start(), calls=%async_computation.1 | async-start | bytes 9437184 | tf_op jit(solution)/shard_map/all_gather | solution.py:102
  39.6 131.3 %copy-start = (s32[16,2]{0,1:T(2,128)S(1)}, s32[16,2]{0,1:T(2,128)}, u32[]{:S(2)}) copy-start(s32[16,2]{0,1:T(2,128)} %param.7) | copy-start | bytes 388
  39.6 131.3 %copy-start.1 = (s32[16]{0:T(128)S(1)}, s32[16]{0:T(128)}, u32[]{:S(2)}) copy-start(s32[16]{0:T(128)} %param.6) | copy-start | bytes 196
Sparse Core Ops, SparseCore 0:
  8.9 30.6 all-gather.2
  117.2 53.6 all-gather.4
where the time goes:
time: 1150 us; the launch traced here: 1140 us
  local copies, waits for them, and re-layouts  684 us (59%)
  matrix products  227 us (20%)
  other arithmetic  102 us (9%)
  waiting for transfers between devices  86.8 us (8%)
  loops' own time  28.1 us (2%)
  between operations  13.4 us (1%)
    gather x1536, local copies, waits for them, and re-layouts  617 us
    dot_general x16, matrix products, one_angle(): jnp.einsum('tsb,tbp->tsp', band_rows, weights, preferred_element_type=jnp...  149 us
    dot_general x1, matrix products, shards(): jnp.dot(whole_bins.reshape(-1, BINS).astype(jnp.float32), ramp_rows, prec...  77.5 us
    all_gather x1, waiting for transfers between devices, shards(): lax.all_gather(filtered, 'ang', axis=0, tiled=True)  53.8 us
    all_gather x1, waiting for transfers between devices, shards(): whole_bins = lax.all_gather(sinogram, 'img', axis=2, tiled=True)  32.3 us
    sub x16, other arithmetic, one_angle(): low_bin = (position // 16 - band_start[:, None])[:, None, :]  31.6 us
    sub x16, other arithmetic, one_angle(): 1.0 - upper_weight  31.3 us
    min x16, other arithmetic, one_angle(): band_start = jnp.minimum(corner // 16, BINS - BAND)  29.1 us
  transfers between devices with their start and end apart: 2, of which 2 were waited for; matrix products, arithmetic and copies ran while one was open for 0% of the time, Pallas kernels for 0%

commit v1 on v0

v1 whole, which is shorter than its diff:
```python
import functools
import math

import jax
import jax.numpy as jnp
from jax import lax
from jax.experimental import pallas as pl
from jax.experimental.pallas import tpu as pltpu
from jax.sharding import PartitionSpec as P

IMG = 1024
STEP_MAX = 32
TILE = 16
BLOCK = 256
LANES = 128
REACH = math.isqrt(2 * STEP_MAX * STEP_MAX)
BAND = -(-(((TILE - 1) * REACH + TILE - 1) // TILE + 2) // 16) * 16


def window_rows(tiles_across, tiles_down):
    far = math.isqrt(STEP_MAX**2 * ((tiles_across - 1) ** 2 + (tiles_down - 1) ** 2))
    return -(-(far + BAND) // 16) * 16


def tile_floor(off, u, v):
    return (off + (TILE - 1) * (jnp.minimum(u, 0) + jnp.minimum(v, 0))) >> 4


def low_corner(u, v, tiles_across, tiles_down):
    return jnp.minimum(u, 0) * (tiles_across - 1) + jnp.minimum(v, 0) * (tiles_down - 1)


def ramp_kernel(bins, hi_ref, lo_ref):
    step = pl.program_id(0)
    shape = hi_ref.shape
    row = lax.broadcasted_iota(jnp.int32, shape, 0)
    col = lax.broadcasted_iota(jnp.int32, shape, 1)
    gap = col - row + (bins - BLOCK) - step * BLOCK
    safe = jnp.where(gap == 0, 1, gap).astype(jnp.float32)
    tail = jnp.where((gap & 1) != 0, -1.0 / (math.pi**2 * safe * safe), 0.0)
    value = jnp.where(gap == 0, 0.25, tail)
    hi = value.astype(jnp.bfloat16)
    hi_ref[...] = hi
    lo_ref[...] = (value - hi.astype(jnp.float32)).astype(jnp.bfloat16)


def ramp_strip(bins):
    blocks = 2 * bins // BLOCK - 1
    mid = bins // BLOCK - 2
    return pl.pallas_call(
        functools.partial(ramp_kernel, bins),
        grid=(blocks,),
        out_specs=[
            pl.BlockSpec((BLOCK, BLOCK), lambda k: (k, 0)),
            pl.BlockSpec((BLOCK, BLOCK), lambda k: (jnp.clip(k - mid, 0, 2), 0)),
        ],
        out_shape=[
            jax.ShapeDtypeStruct((blocks * BLOCK, BLOCK), jnp.bfloat16),
            jax.ShapeDtypeStruct((3 * BLOCK, BLOCK), jnp.bfloat16),
        ],
        cost_estimate=pl.CostEstimate(
            flops=20 * blocks * BLOCK * BLOCK, bytes_accessed=2 * blocks * BLOCK * BLOCK, transcendentals=0
        ),
        name="ramp_strip",
    )()


def filter_kernel(
    targets, tiles_across, tiles_down, win, off_ref, step_ref, hi_ref, lo_ref, x_ref, out_ref, xs_ref, ft_ref
):
    pieces, rows, piece_bins = x_ref.shape
    bins = pieces * piece_bins
    blocks = bins // BLOCK
    edge = jnp.zeros((rows, BLOCK), jnp.bfloat16)
    xs_ref[:, 0:BLOCK] = edge
    xs_ref[:, BLOCK + bins :] = edge
    for q in range(pieces):
        xs_ref[:, BLOCK + q * piece_bins : BLOCK + (q + 1) * piece_bins] = x_ref[q]
    ft_ref[bins:, :] = jnp.zeros((ft_ref.shape[0] - bins, LANES), jnp.float32)

    def one_block(kb, carry):
        start = pl.multiple_of((blocks - 1 - kb) * BLOCK, BLOCK)
        here = pl.multiple_of(kb * BLOCK, BLOCK)
        total = jnp.dot(
            xs_ref[:, BLOCK : BLOCK + bins], hi_ref[pl.ds(start, bins), :], preferred_element_type=jnp.float32
        )
        total += jnp.dot(xs_ref[:, pl.ds(here, 3 * BLOCK)], lo_ref[...], preferred_element_type=jnp.float32)
        for half in range(BLOCK // LANES):
            ft_ref[pl.ds(here + half * LANES, LANES), :] = total[:, half * LANES : (half + 1) * LANES].T
        return carry

    lax.fori_loop(0, blocks, one_block, 0, unroll=2)

    first = lax.axis_index("ang") * 2
    column = lax.axis_index("img")
    lane = lax.broadcasted_iota(jnp.int32, (win, LANES), 1)

    def one_target(t, carry):
        start = []
        for k in range(2):
            u, v = step_ref[first + k, 0], step_ref[first + k, 1]
            start.append(
                tile_floor(off_ref[first + k], u, v)
                + u * (column * tiles_across)
                + v * (t * tiles_down)
                + low_corner(u, v, tiles_across, tiles_down)
            )
        both = jnp.where(lane < LANES // 2, ft_ref[pl.ds(start[0], win), :], ft_ref[pl.ds(start[1], win), :])
        out_ref[t] = both.astype(jnp.bfloat16)
        return carry

    lax.fori_loop(0, targets, one_target, 0)


def filter_windows(pieces, offsets, steps, targets, tiles_across, tiles_down):
    count, rows, piece_bins = pieces.shape
    bins = count * piece_bins
    win = window_rows(tiles_across, tiles_down)
    hi, lo = ramp_strip(bins)
    vmem = pl.BlockSpec(memory_space=pltpu.VMEM)
    smem = pl.BlockSpec(memory_space=pltpu.SMEM)
    return pl.pallas_call(
        functools.partial(filter_kernel, targets, tiles_across, tiles_down, win),
        in_specs=[smem, smem, vmem, vmem, vmem],
        out_specs=vmem,
        out_shape=jax.ShapeDtypeStruct((targets, win, LANES), jnp.bfloat16),
        scratch_shapes=[
            pltpu.VMEM((rows, bins + 2 * BLOCK), jnp.bfloat16),
            pltpu.VMEM((bins + win, LANES), jnp.float32),
        ],
        compiler_params=pltpu.CompilerParams(vmem_limit_bytes=40 * 1024 * 1024),
        cost_estimate=pl.CostEstimate(
            flops=2 * rows * bins * bins, bytes_accessed=4 * bins * BLOCK, transcendentals=0
        ),
        name="filter_windows",
    )(offsets, steps, hi, lo, pieces)


def back_kernel(tiles_across, tiles_down, scale, off_ref, step_ref, w_ref, out_ref, f_ref, r_ref, g_ref, wt_ref, acc_ref):
    pairs, win, _ = w_ref.shape
    angles = 2 * pairs
    half = tiles_down // 2
    margin = STEP_MAX * half
    depth = angles * BAND
    j = pl.program_id(0)

    @pl.when(j == 0)
    def _():
        lane = lax.broadcasted_iota(jnp.int32, (win, LANES), 1)
        low = lane < LANES // 2
        for p in range(pairs):
            whole = w_ref[p].astype(jnp.float32)
            f_ref[margin : margin + win, :] = whole
            r_ref[margin : margin + win, :] = pltpu.roll(whole, LANES // 2, 1)
            jump = [margin + step_ref[2 * p + k, 1] * half for k in range(2)]
            g_ref[2 * p] = jnp.where(low, f_ref[margin : margin + win, :], r_ref[pl.ds(jump[0], win), :])
            g_ref[2 * p + 1] = jnp.where(low, r_ref[margin : margin + win, :], f_ref[pl.ds(jump[1], win), :])
        col = lax.broadcasted_iota(jnp.int32, (1, depth), 1)
        u_row = jnp.zeros((1, depth), jnp.int32)
        v_row = jnp.zeros((1, depth), jnp.int32)
        c_row = jnp.zeros((1, depth), jnp.int32)
        for a in range(angles):
            mine = (col >= a * BAND) & (col < (a + 1) * BAND)
            u, v = step_ref[a, 0], step_ref[a, 1]
            lead = off_ref[a] - TILE * tile_floor(off_ref[a], u, v)
            u_row = jnp.where(mine, u, u_row)
            v_row = jnp.where(mine, v, v_row)
            c_row = jnp.where(mine, lead - TILE * (col - a * BAND), c_row)
        across = lax.broadcasted_iota(jnp.int32, (TILE, depth), 0)
        line = (u_row * across + c_row).astype(jnp.float32)
        v_line = v_row.astype(jnp.float32)
        for y in range(TILE):
            away = jnp.abs(line + v_line * float(y)) * (1.0 / TILE)
            wt_ref[y * TILE : (y + 1) * TILE, :] = jnp.maximum(1.0 - away, 0.0).astype(jnp.bfloat16)

    base = []
    for a in range(angles):
        u, v = step_ref[a, 0], step_ref[a, 1]
        base.append(v * j - low_corner(u, v, tiles_across, tiles_down))

    def two_tiles(ii, carry):
        sides = []
        for e in range(2):
            bands = []
            for a in range(angles):
                start = base[a] + step_ref[a, 0] * (2 * ii + e)
                bands.append(g_ref[a, pl.ds(start, BAND), :].astype(jnp.bfloat16))
            sides.append(jnp.concatenate(bands, axis=0))
        bands = jnp.concatenate(sides, axis=1)
        tile = jnp.dot(wt_ref[...], bands, preferred_element_type=jnp.float32)
        tile = (tile * scale).astype(jnp.bfloat16)
        for e in range(2):
            for y in range(TILE):
                acc_ref[y, pl.ds(pl.multiple_of((2 * ii + e) * TILE, TILE), TILE), :] = tile[
                    y * TILE : (y + 1) * TILE, e * LANES : (e + 1) * LANES
                ]
        return carry

    lax.fori_loop(0, tiles_across // 2, two_tiles, 0, unroll=2)
    slices = LANES // 2
    for y in range(TILE):
        for part in range(tiles_across * TILE // LANES):
            cols = slice(part * LANES, (part + 1) * LANES)
            turned = acc_ref[y, cols, :].T
            out_ref[0, 0, y, :, cols] = turned[0:slices]
            out_ref[1, 0, y, :, cols] = turned[slices:]


def back_project(windows, offsets, steps, tiles_across, tiles_down):
    pairs, win, _ = windows.shape
    angles = 2 * pairs
    half = tiles_down // 2
    cols = tiles_across * TILE
    slices = LANES // 2
    margin = STEP_MAX * half
    smem = pl.BlockSpec(memory_space=pltpu.SMEM)
    scale = 2.0 / math.sqrt(angles)
    out = pl.pallas_call(
        functools.partial(back_kernel, tiles_across, tiles_down, scale),
        grid=(half,),
        in_specs=[smem, smem, pl.BlockSpec(memory_space=pltpu.VMEM)],
        out_specs=pl.BlockSpec((2, 1, TILE, slices, cols), lambda j: (0, j, 0, 0, 0)),
        out_shape=jax.ShapeDtypeStruct((2, half, TILE, slices, cols), jnp.bfloat16),
        scratch_shapes=[
            pltpu.VMEM((win + 2 * margin, LANES), jnp.float32),
            pltpu.VMEM((win + 2 * margin, LANES), jnp.float32),
            pltpu.VMEM((angles, win, LANES), jnp.float32),
            pltpu.VMEM((TILE * TILE, angles * BAND), jnp.bfloat16),
            pltpu.VMEM((TILE, cols, LANES), jnp.bfloat16),
        ],
        compiler_params=pltpu.CompilerParams(vmem_limit_bytes=40 * 1024 * 1024),
        cost_estimate=pl.CostEstimate(
            flops=2 * half * cols * TILE * LANES * angles * BAND, bytes_accessed=4 * half * TILE * slices * cols, transcendentals=0
        ),
        name="back_project",
    )(offsets, steps, windows)
    return out.reshape(tiles_down * TILE, slices, cols)


def shards(sinogram, offsets, steps):
    ang_count = lax.axis_size("ang")
    img_count = lax.axis_size("img")
    tiles_across = IMG // img_count // TILE
    tiles_down = IMG // ang_count // TILE
    angles_dev, slices, piece_bins = sinogram.shape
    pieces = lax.all_gather(sinogram.reshape(angles_dev * slices, piece_bins), "img", axis=0)
    windows = filter_windows(pieces, offsets, steps, ang_count, tiles_across, tiles_down)
    windows = lax.all_to_all(windows, "ang", 0, 0, tiled=True)
    return back_project(windows, offsets, steps, tiles_across, tiles_down)


def solution(mesh):
    return jax.shard_map(
        shards,
        mesh=mesh,
        in_specs=(P("ang", None, "img"), P(), P()),
        out_specs=P("ang", None, "img"),
        check_vma=False,
    )
```

time: 1150 us -> 92.3 us (0.08)
  local copies, waits for them, and re-layouts: 684 us -> 5.78 us
  matrix products: 227 us -> 0 us
  other arithmetic: 102 us -> 0 us
  waiting for transfers between devices: 86.8 us -> 19.5 us
  Pallas kernels: 0 us -> 32.7 us
  loops' own time: 28.1 us -> 0 us
  blocking collectives: 0 us -> 20.6 us
    gather x1536 -> x0, local copies, waits for them, and re-layouts: 617 us -> none
    dot_general x17 -> x0, matrix products: 227 us -> none  [the longest x16 149 us: one_angle(): jnp.einsum('tsb,tbp->tsp', band_rows, weights, preferred_element_type=jnp...]
    all_gather x2 -> x1, waiting for transfers between devices: 86.1 us -> 18.8 us  [shards(): lax.all_gather(sinogram.reshape(angles_dev * slices, piece_bins), 'img',...]
    sub x32 -> x0, other arithmetic: 62.9 us -> none  [the longest x16 31.6 us: one_angle(): low_bin = (position // 16 - band_start[:, None])[:, None, :]]
    pallas_call x0 -> x3, Pallas kernels: none -> 32.7 us  [the longest x1 12.8 us: ramp_strip(): pl.pallas_call(functools.partial(ramp_kernel, bins), grid=(blocks,), out_...]
    min x16 -> x0, other arithmetic: 29.1 us -> none  [one_angle(): band_start = jnp.minimum(corner // 16, BINS - BAND)]
    another operation x17 -> x0, loops' own time: 28.1 us -> none  [the longest x1 20 us: one_block(): lax.scan(one_angle, start_sum, (filtered, geo_offsets, geo_steps))[0]]
    all_to_all x0 -> x1, blocking collectives: none -> 20.6 us  [shards(): windows = lax.all_to_all(windows, 'ang', 0, 0, tiled=True)]
  transfers between devices with their start and end apart: 2 -> 1, of which waited for: 2 -> 1; matrix products, arithmetic and copies ran while one was open for 0% -> 1% of each run, Pallas kernels for 0% -> 14%
where the time goes in v1:
time: 92.3 us; the launch traced here: 92 us
  Pallas kernels  32.7 us (35%)
  blocking collectives  20.6 us (22%)
  waiting for transfers between devices  19.5 us (21%)
  between operations  13.4 us (15%)
  local copies, waits for them, and re-layouts  5.78 us (6%)
    all_to_all x1, blocking collectives, shards(): windows = lax.all_to_all(windows, 'ang', 0, 0, tiled=True)  20.6 us
    all_gather x1, waiting for transfers between devices, shards(): lax.all_gather(sinogram.reshape(angles_dev * slices, piece_bins), 'img',...  18.8 us
    pallas_call x1, Pallas kernels, ramp_strip(): pl.pallas_call(functools.partial(ramp_kernel, bins), grid=(blocks,), out_...  12.8 us
    pallas_call x1, Pallas kernels, back_project(): pl.pallas_call(functools.partial(back_kernel, tiles_across, tiles_down, s...  11.5 us
    pallas_call x1, Pallas kernels, filter_windows(): pl.pallas_call(functools.partial(filter_kernel, targets, tiles_across, ti...  8.46 us
    unnamed x9, local copies, waits for them, and re-layouts  5.78 us
  transfers between devices with their start and end apart: 1, of which 1 were waited for; matrix products, arithmetic and copies ran while one was open for 1% of the time, Pallas kernels for 14%

profile of v1, /device:TPU:0, one launch (start us, length us, event | category | flops | bytes accessed | tf_op | source)
XLA Modules:
  0.0 92.0 jit_solution(3065798192173722315)
XLA Ops:
  6.5 0.0 all-gather.2.cloned.1.call-start
  6.5 0.7 all-gather.2.cloned.1.call-update
  7.3 0.8 copy.7.step_ref
  8.0 12.8 %ramp_strip.1 = (bf16[7936,256]{1,0:T(8,128)(2,1)}, bf16[768,256]{1,0:T(8,128)(2,1)}) custom-call(), custom_call_target="tpu_custom_call" | custom-call | flops 40632320 | bytes 4063232 | tf_op jit(solution)/shard_map/ramp_strip/pallas_call | solution.py:50
  20.8 18.8 %all-gather.2.cloned.1.call-done.x_ref = bf16[4,128,1024]{2,1,0:T(8,128)(2,1)} async-done(((bf16[1,128,1024]{2,1,0:T(8,128)(2,1)}), bf16[4,128,1024]{2,1,0:T(8,128)(2,1)}) %all-gather.2.cloned.1.call-update) | async-done | bytes 1048592 | tf_op jit(solution)/shard_map/all_gather | solution.py:246
  39.6 0.0 copy-start
  39.6 1.2 %copy-done = bf16[4,128,1024]{2,1,0:T(8,128)(2,1)S(1)} copy-done((bf16[4,128,1024]{2,1,0:T(8,128)(2,1)S(1)}, bf16[4,128,1024]{2,1,0:T(8,128)(2,1)}, u32[]{:S(2)}) %copy-start) | copy-done | bytes 1048600
  40.9 0.0 copy-start.1
  40.9 0.7 copy-done.1
  41.5 0.0 copy-start.2
  41.5 2.1 %copy-done.2 = bf16[7936,256]{1,0:T(8,128)(2,1)S(1)} copy-done((bf16[7936,256]{1,0:T(8,128)(2,1)S(1)}, bf16[7936,256]{1,0:T(8,128)(2,1)}, u32[]{:S(2)}) %copy-start.2) | copy-done | bytes 4063256
  43.7 0.0 copy-start.3
  43.7 1.0 %copy-done.3 = bf16[768,256]{1,0:T(8,128)(2,1)S(1)} copy-done((bf16[768,256]{1,0:T(8,128)(2,1)S(1)}, bf16[768,256]{1,0:T(8,128)(2,1)}, u32[]{:S(2)}) %copy-start.3) | copy-done | bytes 393240
  44.7 8.5 %filter_windows.1 = bf16[8,592,128]{2,1,0:T(8,128)(2,1)S(1)} custom-call(s32[16]{0:T(128)S(1)} %copy-done.1, s32[16,2]{1,0:T(8,128)S(1)} %copy.7.step_ref, bf16[7936,256]{1,0:T(8,128)(2,1)S(1)} %copy-done.2, bf16[768,256]{1,0:T(8,128)(2,1)S(1)} %copy-done.3, bf16[4,128,1024]{2,1,0:T(8,128)(2,1)S(1)} %copy-done), custom_call_target="tpu_custom_call" | custom-call | flops 4294967296 | bytes 4194304 | tf_op jit(solution)/shard_map/filter_windows/pallas_call | solution.py:122
  53.1 20.6 %all_to_all.5.w_ref = bf16[8,592,128]{2,1,0:T(8,128)(2,1)S(1)} all-to-all(bf16[8,592,128]{2,1,0:T(8,128)(2,1)S(1)} %filter_windows.1), channel_id=1, replica_groups=mesh['ang'=8,'img'=4] {'ang'}, dimensions={0} | all-to-all | bytes 2424832 | tf_op jit(solution)/shard_map/all_to_all | solution.py:248
  73.7 11.5 %back_project.1 = bf16[2,4,16,64,256]{4,3,2,1,0:T(8,128)(2,1)} custom-call(s32[16]{0:T(128)S(1)} %copy-done.1, s32[16,2]{1,0:T(8,128)S(1)} %copy.7.step_ref, bf16[8,592,128]{2,1,0:T(8,128)(2,1)S(1)} %all_to_all.5.w_ref), custom_call_target="tpu_custom_call" | custom-call | flops 3221225472 | bytes 4194304 | tf_op jit(solution)/shard_map/back_project/pallas_call | solution.py:218
Async XLA Ops:
  6.5 33.1 %all-gather.2.cloned.1.call-start = ((), (), s32[]{:S(2)}) async-start(), calls=%async_computation.1 | async-start | bytes 1310720 | tf_op jit(solution)/shard_map/all_gather | solution.py:246
  39.6 1.2 %copy-start = (bf16[4,128,1024]{2,1,0:T(8,128)(2,1)S(1)}, bf16[4,128,1024]{2,1,0:T(8,128)(2,1)}, u32[]{:S(2)}) copy-start(bf16[4,128,1024]{2,1,0:T(8,128)(2,1)} %all-gather.2.cloned.1.call-done.x_ref) | copy-start | bytes 3145732
  40.9 0.7 copy-start.1
  41.5 2.2 %copy-start.2 = (bf16[7936,256]{1,0:T(8,128)(2,1)S(1)}, bf16[7936,256]{1,0:T(8,128)(2,1)}, u32[]{:S(2)}) copy-start(bf16[7936,256]{1,0:T(8,128)(2,1)} %get-tuple-element.7.hi_ref) | copy-start | bytes 12189700
  43.7 1.0 %copy-start.3 = (bf16[768,256]{1,0:T(8,128)(2,1)S(1)}, bf16[768,256]{1,0:T(8,128)(2,1)}, u32[]{:S(2)}) copy-start(bf16[768,256]{1,0:T(8,128)(2,1)} %get-tuple-element.8.lo_ref) | copy-start | bytes 1179652
Sparse Core Ops, SparseCore 0:
  8.9 30.6 all-gather.1

commit v2 on v1

v2 whole, which is shorter than its diff:
```python
import functools
import math

import jax
import jax.numpy as jnp
import numpy as np
from jax import lax
from jax.experimental import pallas as pl
from jax.experimental.pallas import tpu as pltpu
from jax.sharding import PartitionSpec as P

IMG = 1024
STEP_MAX = 32
TILE = 16
BLOCK = 256
LANES = 128
REACH = math.isqrt(2 * STEP_MAX * STEP_MAX)
BAND = -(-(((TILE - 1) * REACH + TILE - 1) // TILE + 2) // 16) * 16


def window_rows(tiles_across, tiles_down):
    far = math.isqrt(STEP_MAX**2 * ((tiles_across - 1) ** 2 + (tiles_down - 1) ** 2))
    return -(-(far + BAND) // 16) * 16


def tile_floor(off, u, v):
    return (off + (TILE - 1) * (jnp.minimum(u, 0) + jnp.minimum(v, 0))) >> 4


def low_corner(u, v, tiles_across, tiles_down):
    return jnp.minimum(u, 0) * (tiles_across - 1) + jnp.minimum(v, 0) * (tiles_down - 1)


def ramp_strips(bins):
    row = np.arange(2 * bins - LANES)[:, None]
    gap = np.arange(LANES)[None, :] - row + bins - LANES
    safe = np.where(gap == 0, 1, gap).astype(np.float64)
    value = np.where(gap % 2 != 0, -1.0 / (math.pi**2 * safe * safe), 0.0)
    value = np.where(gap == 0, 0.25, value).astype(np.float32)
    hi = value.astype(jnp.bfloat16)
    near = slice(bins - LANES - BLOCK - LANES, bins - LANES + 2 * BLOCK)
    lo = (value[near] - hi[near].astype(np.float32)).astype(jnp.bfloat16)
    return hi, lo


def strip_block(ref, start, depth):
    left = ref[pl.ds(pl.multiple_of(start, LANES), depth), :]
    right = ref[pl.ds(pl.multiple_of(start - LANES, LANES), depth), :]
    return jnp.concatenate([left, right], axis=1)


def early_kernel(early_index, bins, hi_ref, *refs):
    x_refs, part_ref = refs[:-1], refs[-1]
    piece_bins = x_refs[0].shape[1]
    index = early_index(lax.axis_index("img"))

    def one_block(kb, carry):
        total = None
        for q, x_ref in zip(index, x_refs):
            block = strip_block(hi_ref, bins - LANES - kb * BLOCK + q * piece_bins, piece_bins)
            term = jnp.dot(x_ref[...], block, preferred_element_type=jnp.float32)
            total = term if total is None else total + term
        part_ref[kb] = total
        return carry

    lax.fori_loop(0, bins // BLOCK, one_block, 0, unroll=4)


def late_kernel(early_index, late_index, late_source, targets, tiles_across, tiles_down, win, *refs):
    off_ref, step_ref, hi_ref, lo_ref, part_ref = refs[:5]
    xs_ref, ft_ref = refs[-2:]
    out_refs = refs[-2 - targets : -2]
    x_refs = refs[5 : -2 - targets]
    rows, piece_bins = x_refs[0].shape
    blocks = part_ref.shape[0]
    bins = blocks * BLOCK
    here = lax.axis_index("img")
    early, late = early_index(here), late_index(here)
    edge = jnp.zeros((rows, BLOCK), jnp.bfloat16)
    xs_ref[:, 0:BLOCK] = edge
    xs_ref[:, BLOCK + bins :] = edge

    def place(q, x_ref):
        xs_ref[:, pl.ds(pl.multiple_of(BLOCK + q * piece_bins, LANES), piece_bins)] = x_ref[...]

    for q, x_ref in zip(early, x_refs):
        place(q, x_ref)
    for q, choices in zip(late, late_source(here, x_refs[len(early) :])):
        for when, x_ref in choices:
            if when is None:
                place(q, x_ref)
            else:
                pl.when(when)(functools.partial(place, q, x_ref))
    ft_ref[bins:, :] = jnp.zeros((ft_ref.shape[0] - bins, LANES), jnp.float32)

    def one_block(kb, carry):
        first = pl.multiple_of(kb * BLOCK, BLOCK)
        total = part_ref[kb]
        for q in late:
            block = strip_block(hi_ref, bins - LANES - kb * BLOCK + q * piece_bins, piece_bins)
            x = xs_ref[:, pl.ds(pl.multiple_of(BLOCK + q * piece_bins, LANES), piece_bins)]
            total += jnp.dot(x, block, preferred_element_type=jnp.float32)
        total += jnp.dot(
            xs_ref[:, pl.ds(first, 3 * BLOCK)], strip_block(lo_ref, LANES, 3 * BLOCK), preferred_element_type=jnp.float32
        )
        for half in range(BLOCK // LANES):
            ft_ref[pl.ds(first + half * LANES, LANES), :] = total[:, half * LANES : (half + 1) * LANES].T
        return carry

    lax.fori_loop(0, blocks, one_block, 0, unroll=2)

    mine = lax.axis_index("ang")
    lane = lax.broadcasted_iota(jnp.int32, (win, LANES), 1)
    for slot, out_ref in enumerate(out_refs):
        target = (mine >> 1) ^ slot
        start = []
        for k in range(2):
            a = mine * 2 + k
            u, v = step_ref[a, 0], step_ref[a, 1]
            start.append(
                tile_floor(off_ref[a], u, v)
                + u * (here * tiles_across)
                + v * (target * 2 * tiles_down)
                + low_corner(u, v, tiles_across, 2 * tiles_down)
            )
        both = jnp.where(lane < LANES // 2, ft_ref[pl.ds(start[0], win), :], ft_ref[pl.ds(start[1], win), :])
        out_ref[...] = both.astype(jnp.bfloat16)


def gather_plan(block, count):
    if count == 4:
        far = lax.ppermute(block, "img", [(i, i ^ 2) for i in range(4)])
        near = lax.ppermute(block, "img", [(i, i ^ 1) for i in range(4)])
        middle = lax.ppermute(block, "img", [(1, 2), (2, 1)])
        ends = lax.ppermute(far, "img", [(2, 3), (1, 0)])

        def late_source(z, refs):
            inner = (z == 1) | (z == 2)
            return [[(None, refs[0])], [(inner, refs[1]), (jnp.logical_not(inner), refs[2])]]

        return [block, near], [far, middle, ends], lambda z: [z, z ^ 1], lambda z: [z ^ 2, z ^ 3], late_source
    hops = [lax.ppermute(block, "img", [(i, (i + k) % count) for i in range(count)]) for k in range(1, count)]
    source = lambda z, ks: [lax.rem(z + (count - k), count) for k in ks]
    half = count // 2
    return (
        [block] + hops[: half - 1],
        hops[half - 1 :],
        lambda z: source(z, range(half)),
        lambda z: source(z, range(half, count)),
        lambda z, refs: [[(None, ref)] for ref in refs],
    )


def filter_windows(block, offsets, steps, count, targets, tiles_across, tiles_down):
    rows, piece_bins = block.shape
    bins = count * piece_bins
    win = window_rows(tiles_across, 2 * tiles_down)
    hi, lo = (jnp.asarray(x) for x in ramp_strips(bins))
    early, late, early_index, late_index, late_source = gather_plan(block, count)
    vmem = pl.BlockSpec(memory_space=pltpu.VMEM)
    smem = pl.BlockSpec(memory_space=pltpu.SMEM)
    params = pltpu.CompilerParams(vmem_limit_bytes=24 * 1024 * 1024)
    part = pl.pallas_call(
        functools.partial(early_kernel, early_index, bins),
        in_specs=[vmem] * (1 + len(early)),
        out_specs=vmem,
        out_shape=jax.ShapeDtypeStruct((bins // BLOCK, rows, BLOCK), jnp.float32),
        compiler_params=params,
        cost_estimate=pl.CostEstimate(flops=rows * bins * bins, bytes_accessed=8 * bins * LANES, transcendentals=0),
        name="filter_early",
    )(hi, *early)
    return pl.pallas_call(
        functools.partial(late_kernel, early_index, late_index, late_source, targets, tiles_across, tiles_down, win),
        in_specs=[smem, smem] + [vmem] * (3 + len(early) + len(late)),
        out_specs=[vmem] * targets,
        out_shape=[jax.ShapeDtypeStruct((win, LANES), jnp.bfloat16)] * targets,
        scratch_shapes=[
            pltpu.VMEM((rows, bins + 2 * BLOCK), jnp.bfloat16),
            pltpu.VMEM((bins + win, LANES), jnp.float32),
        ],
        compiler_params=params,
        cost_estimate=pl.CostEstimate(flops=rows * bins * bins, bytes_accessed=8 * bins * LANES, transcendentals=0),
        name="filter_late",
    )(offsets, steps, hi, lo, part, *early, *late)


def back_kernel(tiles_across, tiles_down, scale, *refs):
    off_ref, step_ref = refs[:2]
    f_ref, r_ref, g_ref, wt_ref, acc_ref = refs[-5:]
    out_ref, other_ref = refs[-6], refs[-7]
    own_refs = refs[2:-7]
    chips = len(own_refs)
    whole_win = own_refs[0].shape[0]
    win = g_ref.shape[1]
    half = tiles_down // 2
    margin = STEP_MAX * half
    slots = g_ref.shape[0]
    depth = slots * BAND
    j = pl.program_id(0)
    mine = lax.axis_index("ang")
    core = mine & 1

    angle = []
    for side in range(2):
        for c in range(chips):
            pair = ((mine >> 1) ^ c) * 2 + (core ^ side)
            angle += [pair * 2, pair * 2 + 1]
    u = [step_ref[a, 0] for a in angle]
    v = [step_ref[a, 1] for a in angle]

    @pl.when(j == 0)
    def _():
        lane = lax.broadcasted_iota(jnp.int32, (win, LANES), 1)
        low = lane < LANES // 2
        for p in range(slots // 2):
            whole = own_refs[p][...] if p < chips else other_ref[p - chips]
            whole = whole.astype(jnp.float32)
            f_ref[margin : margin + whole_win, :] = whole
            r_ref[margin : margin + whole_win, :] = pltpu.roll(whole, LANES // 2, 1)
            for k, (near, far) in enumerate(((f_ref, r_ref), (r_ref, f_ref))):
                s = 2 * p + k
                start = (
                    margin
                    + v[s] * (core * tiles_down)
                    + low_corner(u[s], v[s], tiles_across, tiles_down)
                    - low_corner(u[s], v[s], tiles_across, 2 * tiles_down)
                )
                g_ref[s] = jnp.where(low, near[pl.ds(start, win), :], far[pl.ds(start + v[s] * half, win), :])
        col = lax.broadcasted_iota(jnp.int32, (1, depth), 1)
        u_row = jnp.zeros((1, depth), jnp.int32)
        v_row = jnp.zeros((1, depth), jnp.int32)
        c_row = jnp.zeros((1, depth), jnp.int32)
        for s in range(slots):
            mask = (col >= s * BAND) & (col < (s + 1) * BAND)
            off = off_ref[angle[s]]
            lead = off - TILE * tile_floor(off, u[s], v[s])
            u_row = jnp.where(mask, u[s], u_row)
            v_row = jnp.where(mask, v[s], v_row)
            c_row = jnp.where(mask, lead - TILE * (col - s * BAND), c_row)
        across = lax.broadcasted_iota(jnp.int32, (TILE, depth), 0)
        line = (u_row * across + c_row).astype(jnp.float32)
        v_line = v_row.astype(jnp.float32)
        for y in range(TILE):
            away = jnp.abs(line + v_line * float(y)) * (1.0 / TILE)
            wt_ref[y * TILE : (y + 1) * TILE, :] = jnp.maximum(1.0 - away, 0.0).astype(jnp.bfloat16)

    base = [v[s] * j - low_corner(u[s], v[s], tiles_across, tiles_down) for s in range(slots)]

    def two_tiles(ii, carry):
        sides = []
        for e in range(2):
            bands = []
            for s in range(slots):
                start = base[s] + u[s] * (2 * ii + e)
                bands.append(g_ref[s, pl.ds(start, BAND), :].astype(jnp.bfloat16))
            sides.append(jnp.concatenate(bands, axis=0))
        bands = jnp.concatenate(sides, axis=1)
        tile = jnp.dot(wt_ref[...], bands, preferred_element_type=jnp.float32)
        tile = (tile * scale).astype(jnp.bfloat16)
        for e in range(2):
            for y in range(TILE):
                acc_ref[y, pl.ds(pl.multiple_of((2 * ii + e) * TILE, TILE), TILE), :] = tile[
                    y * TILE : (y + 1) * TILE, e * LANES : (e + 1) * LANES
                ]
        return carry

    lax.fori_loop(0, tiles_across // 2, two_tiles, 0, unroll=2)
    slices = LANES // 2
    for y in range(TILE):
        for part in range(tiles_across * TILE // LANES):
            cols = slice(part * LANES, (part + 1) * LANES)
            turned = acc_ref[y, cols, :].T
            out_ref[0, 0, y, :, cols] = turned[0:slices]
            out_ref[1, 0, y, :, cols] = turned[slices:]


def back_project(own, other, offsets, steps, tiles_across, tiles_down):
    chips = len(own)
    slots = 4 * chips
    win = window_rows(tiles_across, tiles_down)
    half = tiles_down // 2
    cols = tiles_across * TILE
    slices = LANES // 2
    margin = STEP_MAX * half
    smem = pl.BlockSpec(memory_space=pltpu.SMEM)
    vmem = pl.BlockSpec(memory_space=pltpu.VMEM)
    scale = 2.0 / math.sqrt(slots)
    padded = own[0].shape[0] + 2 * margin + win
    out = pl.pallas_call(
        functools.partial(back_kernel, tiles_across, tiles_down, scale),
        grid=(half,),
        in_specs=[smem, smem] + [vmem] * (chips + 1),
        out_specs=pl.BlockSpec((2, 1, TILE, slices, cols), lambda j: (0, j, 0, 0, 0)),
        out_shape=jax.ShapeDtypeStruct((2, half, TILE, slices, cols), jnp.bfloat16),
        scratch_shapes=[
            pltpu.VMEM((padded, LANES), jnp.float32),
            pltpu.VMEM((padded, LANES), jnp.float32),
            pltpu.VMEM((slots, win, LANES), jnp.float32),
            pltpu.VMEM((TILE * TILE, slots * BAND), jnp.bfloat16),
            pltpu.VMEM((TILE, cols, LANES), jnp.bfloat16),
        ],
        compiler_params=pltpu.CompilerParams(vmem_limit_bytes=24 * 1024 * 1024),
        cost_estimate=pl.CostEstimate(
            flops=2 * half * cols * TILE * LANES * slots * BAND, bytes_accessed=4 * half * TILE * slices * cols, transcendentals=0
        ),
        name="back_project",
    )(offsets, steps, *own, other)
    return out.reshape(tiles_down * TILE, slices, cols)


def shards(sinogram, offsets, steps):
    ang_count = lax.axis_size("ang")
    img_count = lax.axis_size("img")
    tiles_across = IMG // img_count // TILE
    tiles_down = IMG // ang_count // TILE
    angles_dev, slices, piece_bins = sinogram.shape
    block = sinogram.reshape(angles_dev * slices, piece_bins)
    chips = ang_count // 2
    windows = filter_windows(block, offsets, steps, img_count, chips, tiles_across, tiles_down)
    own = [windows[0]]
    for slot in range(1, chips):
        own.append(lax.ppermute(windows[slot], "ang", [(i, i ^ (2 * slot)) for i in range(ang_count)]))
    other = lax.ppermute(jnp.stack(own), "ang", [(i, i ^ 1) for i in range(ang_count)])
    return back_project(own, other, offsets, steps, tiles_across, tiles_down)


def solution(mesh):
    return jax.shard_map(
        shards,
        mesh=mesh,
        in_specs=(P("ang", None, "img"), P(), P()),
        out_specs=P("ang", None, "img"),
        check_vma=False,
    )
```

time: 92.3 us -> 57.4 us (0.62)
  the two profiles are of different devices: /device:TPU:0 before, /device:TPU:17 now
where the time goes in v2:
time: 57.4 us; the launch traced here: 57.2 us
  Pallas kernels  21.3 us (37%)
  waiting for transfers between devices  16.4 us (29%)
  starting transfers between devices  16.1 us (28%)
  local copies, waits for them, and re-layouts  3.29 us (6%)
    pallas_call x1, Pallas kernels, back_project(): pl.pallas_call(functools.partial(back_kernel, tiles_across, tiles_down, s...  12 us
    ppermute x3, waiting for transfers between devices, shards(): lax.ppermute(windows[slot], 'ang', [(i, i ^ 2 * slot) for i in range(ang_...  7.81 us
    ppermute x1, starting transfers between devices, gather_plan(): ends = lax.ppermute(far, 'img', [(2, 3), (1, 0)])  6.79 us
    ppermute x1, waiting for transfers between devices, gather_plan(): far = lax.ppermute(block, 'img', [(i, i ^ 2) for i in range(4)])  6.7 us
    pallas_call x1, Pallas kernels, filter_windows(): pl.pallas_call(functools.partial(late_kernel, early_index, late_index, la...  6.38 us
    unnamed x9, local copies, waits for them, and re-layouts  3.29 us
    ppermute x1, starting transfers between devices, gather_plan(): middle = lax.ppermute(block, 'img', [(1, 2), (2, 1)])  3.19 us
    pallas_call x1, Pallas kernels, filter_windows(): pl.pallas_call(functools.partial(early_kernel, early_index, bins), in_spe...  2.9 us
  transfers between devices with their start and end apart: 8, of which 5 were waited for; matrix products, arithmetic and copies ran while one was open for 1% of the time, Pallas kernels for 5%

profile of v2, /device:TPU:17, one launch (start us, length us, event | category | flops | bytes accessed | tf_op | source)
XLA Modules:
  0.0 57.2 jit_solution(12871747036073842213)
XLA Ops:
  0.0 0.0 collective-permute-start.1
  0.0 1.3 %collective-permute-start = (bf16[128,1024]{1,0:T(8,128)(2,1)}, bf16[128,1024]{1,0:T(8,128)(2,1)S(1)}, u32[]{:S(2)}, u32[]{:S(2)}) collective-permute-start(bf16[128,1024]{1,0:T(8,128)(2,1)} %bitcast.11), channel_id=1, source_target_pairs={{0,1},{1,0},{2,3},{3,2},{4,5},{5,4},{6,7},{7,6},{8,9},{9,8},{10,11... | collective-permute-start | bytes 786440 | tf_op jit(solution)/shard_map/ppermute | solution.py:133
  1.4 3.2 %collective-permute-start.2 = (bf16[128,1024]{1,0:T(8,128)(2,1)}, bf16[128,1024]{1,0:T(8,128)(2,1)S(1)}, u32[]{:S(2)}, u32[]{:S(2)}) collective-permute-start(bf16[128,1024]{1,0:T(8,128)(2,1)} %bitcast.12), channel_id=1, source_target_pairs={{1,2},{2,1},{5,6},{6,5},{9,10},{10,9},{13,14},{14,13},{17,18},{18,... | collective-permute-start | bytes 786440 | tf_op jit(solution)/shard_map/ppermute | solution.py:134
  4.6 6.7 %collective-permute-done.1.refs_7_ = bf16[128,1024]{1,0:T(8,128)(2,1)S(1)} collective-permute-done((bf16[128,1024]{1,0:T(8,128)(2,1)}, bf16[128,1024]{1,0:T(8,128)(2,1)S(1)}, u32[]{:S(2)}, u32[]{:S(2)}) %collective-permute-start.1) | collective-permute-done | bytes 262176 | tf_op jit(solution)/shard_map/ppermute | solution.py:132
  11.3 6.8 %collective-permute-start.3 = (bf16[128,1024]{1,0:T(8,128)(2,1)S(1)}, bf16[128,1024]{1,0:T(8,128)(2,1)S(1)}, u32[]{:S(2)}, u32[]{:S(2)}) collective-permute-start(bf16[128,1024]{1,0:T(8,128)(2,1)S(1)} %collective-permute-done.1.refs_7_), channel_id=1, source_target_pairs={{2,3},{1,0},{6,7},{5,4},{10,11},{9,8},{14,15},{13,12},{18,19},{17,... | collective-permute-start | bytes 786440 | tf_op jit(solution)/shard_map/ppermute | solution.py:135
  18.1 0.8 %copy.7.refs_1_ = s32[16,2]{1,0:T(8,128)S(1)} copy(s32[16,2]{0,1:T(2,128)} %param.7) | data formatting | bytes 256 | tf_op args[2]
  18.8 0.0 collective-permute-done.refs_1_.refs_6_
  18.8 0.9 %copy-done = bf16[2,64,1024]{2,1,0:T(8,128)(2,1)S(1)} copy-done((bf16[2,64,1024]{2,1,0:T(8,128)(2,1)S(1)}, bf16[2,64,1024]{2,1,0:T(8,128)(2,1)}, u32[]{:S(2)}) %copy-start) | copy-done | bytes 262168
  19.8 1.6 %copy-done.2 = bf16[8064,128]{1,0:T(8,128)(2,1)S(1)} copy-done((bf16[8064,128]{1,0:T(8,128)(2,1)S(1)}, bf16[8064,128]{1,0:T(8,128)(2,1)}, u32[]{:S(2)}) %copy-start.2) | copy-done | bytes 2064408
  21.4 2.9 %filter_early.1.refs_4_ = f32[16,128,256]{2,1,0:T(8,128)S(1)} custom-call(bf16[8064,128]{1,0:T(8,128)(2,1)S(1)} %copy-done.2, bf16[128,1024]{1,0:T(8,128)(2,1)S(1)} %bitcast.13, bf16[128,1024]{1,0:T(8,128)(2,1)S(1)} %collective-permute-done.refs_1_.refs_6_), custom_call_target="tpu_custom_call" | custom-call | flops 2147483648 | bytes 4194304 | tf_op jit(solution)/shard_map/filter_early/pallas_call | solution.py:163
  24.3 0.0 collective-permute-done.2.refs_8_
  24.3 0.0 collective-permute-done.3.refs_9_
  24.3 0.0 copy-done.1
  24.3 6.4 %filter_late.1 = (bf16[736,128]{1,0:T(8,128)(2,1)S(1)}, bf16[736,128]{1,0:T(8,128)(2,1)S(1)}, bf16[736,128]{1,0:T(8,128)(2,1)S(1)}, bf16[736,128]{1,0:T(8,128)(2,1)S(1)}) custom-call(s32[16]{0:T(128)S(1)} %copy-done.1, s32[16,2]{1,0:T(8,128)S(1)} %copy.7.refs_1_, bf16[8064,128]{1,0:T(8,128)(2,1)S(1)} %copy-done.2, bf16[896,128]{1,0:T(8,128)(2,1)S(1)} %copy-done.3, ...), custom_call_target="tpu_custom_call" | custom-call | flops 2147483648 | bytes 4194304 | tf_op jit(solution)/shard_map/filter_late/pallas_call | solution.py:172
  30.7 1.3 %collective-permute-start.4 = (bf16[736,128]{1,0:T(8,128)(2,1)S(1)}, bf16[736,128]{1,0:T(8,128)(2,1)S(1)}, u32[]{:S(2)}, u32[]{:S(2)}) collective-permute-start(bf16[736,128]{1,0:T(8,128)(2,1)S(1)} %get-tuple-element.10), channel_id=1, source_target_pairs={{0,8},{4,12},{8,0},{12,4},{16,24},{20,28},{24,16},{28,20},{1,9},{5... | collective-permute-start | bytes 565256 | tf_op jit(solution)/shard_map/ppermute | solution.py:322
  32.0 1.2 %collective-permute-start.5 = (bf16[736,128]{1,0:T(8,128)(2,1)S(1)}, bf16[736,128]{1,0:T(8,128)(2,1)S(1)}, u32[]{:S(2)}, u32[]{:S(2)}) collective-permute-start(bf16[736,128]{1,0:T(8,128)(2,1)S(1)} %get-tuple-element.11), channel_id=1, source_target_pairs={{0,16},{4,20},{8,24},{12,28},{16,0},{20,4},{24,8},{28,12},{1,17},{... | collective-permute-start | bytes 565256 | tf_op jit(solution)/shard_map/ppermute | solution.py:322
  33.1 0.2 collective-permute-start.6
  33.4 2.8 %collective-permute-done.4.refs_3_ = bf16[736,128]{1,0:T(8,128)(2,1)S(1)} collective-permute-done((bf16[736,128]{1,0:T(8,128)(2,1)S(1)}, bf16[736,128]{1,0:T(8,128)(2,1)S(1)}, u32[]{:S(2)}, u32[]{:S(2)}) %collective-permute-start.4) | collective-permute-done | bytes 188448 | tf_op jit(solution)/shard_map/ppermute | solution.py:322
  36.2 1.0 %collective-permute-done.5.refs_4_ = bf16[736,128]{1,0:T(8,128)(2,1)S(1)} collective-permute-done((bf16[736,128]{1,0:T(8,128)(2,1)S(1)}, bf16[736,128]{1,0:T(8,128)(2,1)S(1)}, u32[]{:S(2)}, u32[]{:S(2)}) %collective-permute-start.5) | collective-permute-done | bytes 188448 | tf_op jit(solution)/shard_map/ppermute | solution.py:322
  37.2 4.0 %collective-permute-done.6.refs_5_ = bf16[736,128]{1,0:T(8,128)(2,1)S(1)} collective-permute-done((bf16[736,128]{1,0:T(8,128)(2,1)S(1)}, bf16[736,128]{1,0:T(8,128)(2,1)S(1)}, u32[]{:S(2)}, u32[]{:S(2)}) %collective-permute-start.6) | collective-permute-done | bytes 188448 | tf_op jit(solution)/shard_map/ppermute | solution.py:322
  41.2 0.1 pad_maximum_fusion
  41.3 2.0 %collective-permute-start.7 = (bf16[4,736,128]{2,1,0:T(8,128)(2,1)S(1)}, bf16[4,736,128]{2,1,0:T(8,128)(2,1)S(1)}, u32[]{:S(2)}, u32[]{:S(2)}) collective-permute-start(bf16[4,736,128]{2,1,0:T(8,128)(2,1)S(1)} %pad_maximum_fusion), channel_id=1, source_target_pairs={{0,4},{4,0},{8,12},{12,8},{16,20},{20,16},{24,28},{28,24},{1,5},{5... | collective-permute-start | bytes 2261000 | tf_op jit(solution)/shard_map/ppermute | solution.py:323
  43.3 1.9 %collective-permute-done.7.refs_6_ = bf16[4,736,128]{2,1,0:T(8,128)(2,1)S(1)} collective-permute-done((bf16[4,736,128]{2,1,0:T(8,128)(2,1)S(1)}, bf16[4,736,128]{2,1,0:T(8,128)(2,1)S(1)}, u32[]{:S(2)}, u32[]{:S(2)}) %collective-permute-start.7) | collective-permute-done | bytes 753696 | tf_op jit(solution)/shard_map/ppermute | solution.py:323
  45.2 12.0 %back_project.1 = bf16[2,4,16,64,256]{4,3,2,1,0:T(8,128)(2,1)} custom-call(s32[16]{0:T(128)S(1)} %copy-done.1, s32[16,2]{1,0:T(8,128)S(1)} %copy.7.refs_1_, bf16[736,128]{1,0:T(8,128)(2,1)S(1)} %get-tuple-element.9.refs_2_, bf16[736,128]{1,0:T(8,128)(2,1)S(1)} %collective-permute-done.4.refs_3_, bf16[736,128]{1,0:T(8,128)(2,1)S(1)} %collective-permute-done.5.refs_4_, ...), custom_call_target="tpu_custom_call" | custom-call | flops 3221225472 | bytes 4194304 | tf_op jit(solution)/shard_map/back_project/pallas_call | solution.py:289
  (5 shorter events, 0.0 us)
Async XLA Ops:
  0.0 11.3 %collective-permute-start.1 = (bf16[128,1024]{1,0:T(8,128)(2,1)}, bf16[128,1024]{1,0:T(8,128)(2,1)S(1)}, u32[]{:S(2)}, u32[]{:S(2)}) collective-permute-start(bf16[128,1024]{1,0:T(8,128)(2,1)} %bitcast.10), channel_id=1, source_target_pairs={{0,2},{1,3},{2,0},{3,1},{4,6},{5,7},{6,4},{7,5},{8,10},{9,11},{10,... | collective-permute-start | bytes 786440 | tf_op jit(solution)/shard_map/ppermute | solution.py:132
  0.0 18.8 %collective-permute-start = (bf16[128,1024]{1,0:T(8,128)(2,1)}, bf16[128,1024]{1,0:T(8,128)(2,1)S(1)}, u32[]{:S(2)}, u32[]{:S(2)}) collective-permute-start(bf16[128,1024]{1,0:T(8,128)(2,1)} %bitcast.11), channel_id=1, source_target_pairs={{0,1},{1,0},{2,3},{3,2},{4,5},{5,4},{6,7},{7,6},{8,9},{9,8},{10,11... | collective-permute-start | bytes 786440 | tf_op jit(solution)/shard_map/ppermute | solution.py:133
  1.4 22.9 %collective-permute-start.2 = (bf16[128,1024]{1,0:T(8,128)(2,1)}, bf16[128,1024]{1,0:T(8,128)(2,1)S(1)}, u32[]{:S(2)}, u32[]{:S(2)}) collective-permute-start(bf16[128,1024]{1,0:T(8,128)(2,1)} %bitcast.12), channel_id=1, source_target_pairs={{1,2},{2,1},{5,6},{6,5},{9,10},{10,9},{13,14},{14,13},{17,18},{18,... | collective-permute-start | bytes 786440 | tf_op jit(solution)/shard_map/ppermute | solution.py:134
  11.3 13.0 %collective-permute-start.3 = (bf16[128,1024]{1,0:T(8,128)(2,1)S(1)}, bf16[128,1024]{1,0:T(8,128)(2,1)S(1)}, u32[]{:S(2)}, u32[]{:S(2)}) collective-permute-start(bf16[128,1024]{1,0:T(8,128)(2,1)S(1)} %collective-permute-done.1.refs_7_), channel_id=1, source_target_pairs={{2,3},{1,0},{6,7},{5,4},{10,11},{9,8},{14,15},{13,12},{18,19},{17,... | collective-permute-start | bytes 786440 | tf_op jit(solution)/shard_map/ppermute | solution.py:135
  18.8 1.0 %copy-start = (bf16[2,64,1024]{2,1,0:T(8,128)(2,1)S(1)}, bf16[2,64,1024]{2,1,0:T(8,128)(2,1)}, u32[]{:S(2)}) copy-start(bf16[2,64,1024]{2,1,0:T(8,128)(2,1)} %param.5) | copy-start | bytes 786436
  19.8 1.6 %copy-start.2 = (bf16[8064,128]{1,0:T(8,128)(2,1)S(1)}, bf16[8064,128]{1,0:T(8,128)(2,1)}, u32[]{:S(2)}) copy-start(bf16[8064,128]{1,0:T(8,128)(2,1)} %constant.4.clone.hi_ref.refs_2_) | copy-start | bytes 6193156
  21.3 2.9 %copy-start.1 = (s32[16]{0:T(128)S(1)}, s32[16]{0:T(128)}, u32[]{:S(2)}) copy-start(s32[16]{0:T(128)} %refs_0_.3) | copy-start | bytes 196
  21.3 2.9 %copy-start.3 = (bf16[896,128]{1,0:T(8,128)(2,1)S(1)}, bf16[896,128]{1,0:T(8,128)(2,1)}, u32[]{:S(2)}) copy-start(bf16[896,128]{1,0:T(8,128)(2,1)} %constant.5.clone.refs_3_) | copy-start | bytes 688132
  30.7 5.5 %collective-permute-start.4 = (bf16[736,128]{1,0:T(8,128)(2,1)S(1)}, bf16[736,128]{1,0:T(8,128)(2,1)S(1)}, u32[]{:S(2)}, u32[]{:S(2)}) collective-permute-start(bf16[736,128]{1,0:T(8,128)(2,1)S(1)} %get-tuple-element.10), channel_id=1, source_target_pairs={{0,8},{4,12},{8,0},{12,4},{16,24},{20,28},{24,16},{28,20},{1,9},{5... | collective-permute-start | bytes 565256 | tf_op jit(solution)/shard_map/ppermute | solution.py:322
  32.0 5.2 %collective-permute-start.5 = (bf16[736,128]{1,0:T(8,128)(2,1)S(1)}, bf16[736,128]{1,0:T(8,128)(2,1)S(1)}, u32[]{:S(2)}, u32[]{:S(2)}) collective-permute-start(bf16[736,128]{1,0:T(8,128)(2,1)S(1)} %get-tuple-element.11), channel_id=1, source_target_pairs={{0,16},{4,20},{8,24},{12,28},{16,0},{20,4},{24,8},{28,12},{1,17},{... | collective-permute-start | bytes 565256 | tf_op jit(solution)/shard_map/ppermute | solution.py:322
  33.1 8.1 %collective-permute-start.6 = (bf16[736,128]{1,0:T(8,128)(2,1)S(1)}, bf16[736,128]{1,0:T(8,128)(2,1)S(1)}, u32[]{:S(2)}, u32[]{:S(2)}) collective-permute-start(bf16[736,128]{1,0:T(8,128)(2,1)S(1)} %get-tuple-element.12), channel_id=1, source_target_pairs={{0,24},{4,28},{8,16},{12,20},{16,8},{20,12},{24,0},{28,4},{1,25},{... | collective-permute-start | bytes 565256 | tf_op jit(solution)/shard_map/ppermute | solution.py:322
  41.3 3.9 %collective-permute-start.7 = (bf16[4,736,128]{2,1,0:T(8,128)(2,1)S(1)}, bf16[4,736,128]{2,1,0:T(8,128)(2,1)S(1)}, u32[]{:S(2)}, u32[]{:S(2)}) collective-permute-start(bf16[4,736,128]{2,1,0:T(8,128)(2,1)S(1)} %pad_maximum_fusion), channel_id=1, source_target_pairs={{0,4},{4,0},{8,12},{12,8},{16,20},{20,16},{24,28},{28,24},{1,5},{5... | collective-permute-start | bytes 2261000 | tf_op jit(solution)/shard_map/ppermute | solution.py:323

commit v3 on v2

v3 whole, which is shorter than its diff:
```python
import functools
import math

import jax
import jax.numpy as jnp
import numpy as np
from jax import lax
from jax.experimental import pallas as pl
from jax.experimental.pallas import tpu as pltpu
from jax.sharding import PartitionSpec as P

IMG = 1024
STEP_MAX = 32
TILE = 16
BLOCK = 256
LANES = 128
REACH = math.isqrt(2 * STEP_MAX * STEP_MAX)
BAND = -(-(((TILE - 1) * REACH + TILE - 1) // TILE + 2) // 16) * 16


def window_rows(tiles_across, tiles_down):
    far = math.isqrt(STEP_MAX**2 * ((tiles_across - 1) ** 2 + (tiles_down - 1) ** 2))
    return -(-(far + BAND) // 16) * 16


def tile_floor(off, u, v):
    return (off + (TILE - 1) * (jnp.minimum(u, 0) + jnp.minimum(v, 0))) >> 4


def low_corner(u, v, tiles_across, tiles_down):
    return jnp.minimum(u, 0) * (tiles_across - 1) + jnp.minimum(v, 0) * (tiles_down - 1)


def ramp_strips(bins):
    row = np.arange(2 * bins - LANES)[:, None]
    gap = np.arange(LANES)[None, :] - row + bins - LANES
    safe = np.where(gap == 0, 1, gap).astype(np.float64)
    value = np.where(gap % 2 != 0, -1.0 / (math.pi**2 * safe * safe), 0.0)
    value = np.where(gap == 0, 0.25, value).astype(np.float32)
    hi = value.astype(jnp.bfloat16)
    near = slice(bins - 3 * LANES, bins - LANES + BLOCK + LANES)
    lo = (value[near] - hi[near].astype(np.float32)).astype(jnp.bfloat16)
    return hi, lo


def strip_block(ref, start, depth):
    left = ref[pl.ds(pl.multiple_of(start, LANES), depth), :]
    right = ref[pl.ds(pl.multiple_of(start - LANES, LANES), depth), :]
    return jnp.concatenate([left, right], axis=1)


def lanes_of(q, piece_bins):
    return pl.ds(pl.multiple_of(BLOCK + q * piece_bins, LANES), piece_bins)


def partial_kernel(index, bins, seeded, hi_ref, *refs):
    x_refs, part_ref = refs[seeded:-1], refs[-1]
    piece_bins = x_refs[0].shape[1]
    index = index(lax.axis_index("img"))

    def one_block(kb, carry):
        total = refs[0][kb] if seeded else None
        for q, x_ref in zip(index, x_refs):
            block = strip_block(hi_ref, bins - LANES - kb * BLOCK + q * piece_bins, piece_bins)
            term = jnp.dot(x_ref[...], block, preferred_element_type=jnp.float32)
            total = term if total is None else total + term
        part_ref[kb] = total
        return carry

    lax.fori_loop(0, bins // BLOCK, one_block, 0, unroll=4)


def late_kernel(plan, targets, tiles_across, tiles_down, win, *refs):
    off_ref, step_ref, hi_ref, lo_ref, part_ref = refs[:5]
    xs_ref, ft_ref = refs[-2:]
    out_refs = refs[-2 - targets : -2]
    x_refs = refs[5 : -2 - targets]
    rows, piece_bins = x_refs[0].shape
    blocks = part_ref.shape[0]
    bins = blocks * BLOCK
    here = lax.axis_index("img")
    edge = jnp.zeros((rows, BLOCK), jnp.bfloat16)
    xs_ref[:, 0:BLOCK] = edge
    xs_ref[:, BLOCK + bins :] = edge

    def place(q, x_ref):
        xs_ref[:, lanes_of(q, piece_bins)] = x_ref[...]

    for when, q, x_ref in plan(here, x_refs):
        if when is None:
            place(q, x_ref)
        else:
            pl.when(when)(functools.partial(place, q, x_ref))
    last = plan(here, x_refs)[-1][1]
    ft_ref[bins:, :] = jnp.zeros((ft_ref.shape[0] - bins, LANES), jnp.float32)

    def one_block(kb, carry):
        first = pl.multiple_of(kb * BLOCK, BLOCK)
        near = pl.ds(pl.multiple_of(first + BLOCK - LANES, LANES), BLOCK + 2 * LANES)
        total = part_ref[kb]
        block = strip_block(hi_ref, bins - LANES - kb * BLOCK + last * piece_bins, piece_bins)
        total += jnp.dot(xs_ref[:, lanes_of(last, piece_bins)], block, preferred_element_type=jnp.float32)
        total += jnp.dot(
            xs_ref[:, near], strip_block(lo_ref, LANES, BLOCK + 2 * LANES), preferred_element_type=jnp.float32
        )
        for half in range(BLOCK // LANES):
            ft_ref[pl.ds(first + half * LANES, LANES), :] = total[:, half * LANES : (half + 1) * LANES].T
        return carry

    lax.fori_loop(0, blocks, one_block, 0, unroll=4)

    mine = lax.axis_index("ang")
    chunk = 16
    low = lax.broadcasted_iota(jnp.int32, (chunk, LANES), 1) < LANES // 2
    for slot in reversed(range(targets)):
        target = (mine >> 1) ^ slot
        start = []
        for k in range(2):
            a = mine * 2 + k
            u, v = step_ref[0, a], step_ref[1, a]
            start.append(
                tile_floor(off_ref[a], u, v)
                + u * (here * tiles_across)
                + v * (target * 2 * tiles_down)
                + low_corner(u, v, tiles_across, 2 * tiles_down)
            )
        for r in range(0, win, chunk):
            first, second = (ft_ref[pl.ds(at + r, chunk), :] for at in start)
            out_refs[slot][r : r + chunk, :] = jnp.where(low, first, second).astype(jnp.bfloat16)


def filter_windows(block, offsets, steps, count, targets, tiles_across, tiles_down):
    rows, piece_bins = block.shape
    bins = count * piece_bins
    win = window_rows(tiles_across, 2 * tiles_down)
    hi, lo = (jnp.asarray(x) for x in ramp_strips(bins))
    vmem = pl.BlockSpec(memory_space=pltpu.VMEM)
    smem = pl.BlockSpec(memory_space=pltpu.SMEM)
    params = pltpu.CompilerParams(vmem_limit_bytes=20 * 1024 * 1024)

    def partial(index, pieces, part=None):
        seed = [] if part is None else [part]
        return pl.pallas_call(
            functools.partial(partial_kernel, index, bins, len(seed)),
            in_specs=[vmem] * (1 + len(seed) + len(pieces)),
            out_specs=vmem,
            out_shape=jax.ShapeDtypeStruct((bins // BLOCK, rows, BLOCK), jnp.float32),
            compiler_params=params,
            cost_estimate=pl.CostEstimate(
                flops=2 * rows * bins * piece_bins * len(pieces), bytes_accessed=8 * bins * LANES, transcendentals=0
            ),
            name="filter_part%d" % len(pieces),
        )(hi, *seed, *pieces)

    def send(x, pairs):
        return lax.ppermute(x, "img", pairs)

    if count == 4:
        far = send(block, [(i, i ^ 2) for i in range(4)])
        near = send(block, [(i, i ^ 1) for i in range(4)])
        part = partial(lambda z: [z, z ^ 1], [block, near])
        far, again, part = lax.optimization_barrier((far, block, part))
        ends = send(far, [(2, 3), (1, 0)])
        middle = send(again, [(1, 2), (2, 1)])
        part = partial(lambda z: [z ^ 2], [far], part)
        pieces = [block, near, far, middle, ends]

        def plan(z, refs):
            inner = (z == 1) | (z == 2)
            return [
                (None, z, refs[0]),
                (None, z ^ 1, refs[1]),
                (None, z ^ 2, refs[2]),
                (inner, z ^ 3, refs[3]),
                (jnp.logical_not(inner), z ^ 3, refs[4]),
            ]
    else:
        pieces = [block] + [send(block, [(i, (i + k) % count) for i in range(count)]) for k in range(1, count)]
        part = partial(lambda z: [lax.rem(z + (count - k), count) for k in range(count - 1)], pieces[:-1])

        def plan(z, refs):
            return [(None, lax.rem(z + (count - k), count), ref) for k, ref in enumerate(refs)]

    return pl.pallas_call(
        functools.partial(late_kernel, plan, targets, tiles_across, tiles_down, win),
        in_specs=[smem, smem] + [vmem] * (3 + len(pieces)),
        out_specs=[vmem] * targets,
        out_shape=[jax.ShapeDtypeStruct((win, LANES), jnp.bfloat16)] * targets,
        scratch_shapes=[
            pltpu.VMEM((rows, bins + 2 * BLOCK), jnp.bfloat16),
            pltpu.VMEM((bins + win, LANES), jnp.float32),
        ],
        compiler_params=params,
        cost_estimate=pl.CostEstimate(
            flops=3 * rows * bins * piece_bins, bytes_accessed=8 * bins * LANES, transcendentals=0
        ),
        name="filter_late",
    )(offsets, steps, hi, lo, part, *pieces)


def slot_angles(side, chips):
    mine = lax.axis_index("ang")
    angles = []
    for c in range(chips):
        pair = ((mine >> 1) ^ c) * 2 + ((mine & 1) ^ side)
        angles += [pair * 2, pair * 2 + 1]
    return angles


def spread(windows, angles, step_ref, tiles_across, tiles_down, win, g_ref, scratch):
    half = tiles_down // 2
    margin = STEP_MAX * half
    core = lax.axis_index("ang") & 1
    chunk = 16
    low = lax.broadcasted_iota(jnp.int32, (chunk, LANES), 1) < LANES // 2
    for p, window in enumerate(windows):
        f_ref, r_ref = scratch[2 * (p % 2) : 2 * (p % 2) + 2]
        for r in range(0, window.shape[0], chunk):
            rows = window[r : r + chunk, :].astype(jnp.float32)
            f_ref[margin + r : margin + r + chunk, :] = rows
            r_ref[margin + r : margin + r + chunk, :] = pltpu.roll(rows, LANES // 2, 1)
        for k, (near, far) in enumerate(((f_ref, r_ref), (r_ref, f_ref))):
            s = 2 * p + k
            u, v = step_ref[0, angles[s]], step_ref[1, angles[s]]
            start = (
                margin
                + v * (core * tiles_down)
                + low_corner(u, v, tiles_across, tiles_down)
                - low_corner(u, v, tiles_across, 2 * tiles_down)
            )
            for r in range(0, win, chunk):
                g_ref[s, r : r + chunk, :] = jnp.where(
                    low, near[pl.ds(start + r, chunk), :], far[pl.ds(start + v * half + r, chunk), :]
                )


def own_kernel(tiles_across, tiles_down, win, *refs):
    off_ref, step_ref = refs[:2]
    g_ref, wt_ref = refs[-6:-4]
    windows = refs[2:-6]
    chips = len(windows)
    own = slot_angles(0, chips)
    spread(windows, own, step_ref, tiles_across, tiles_down, win, g_ref, refs[-4:])
    angles = own + slot_angles(1, chips)
    depth = len(angles) * BAND
    col = lax.broadcasted_iota(jnp.int32, (1, depth), 1)
    u_row = jnp.zeros((1, depth), jnp.int32)
    v_row = jnp.zeros((1, depth), jnp.int32)
    c_row = jnp.zeros((1, depth), jnp.int32)
    for s, a in enumerate(angles):
        mask = (col >= s * BAND) & (col < (s + 1) * BAND)
        u, v, off = step_ref[0, a], step_ref[1, a], off_ref[a]
        lead = off - TILE * tile_floor(off, u, v)
        u_row = jnp.where(mask, u, u_row)
        v_row = jnp.where(mask, v, v_row)
        c_row = jnp.where(mask, lead - TILE * (col - s * BAND), c_row)
    across = lax.broadcasted_iota(jnp.int32, (TILE, depth), 0)
    line = (u_row * across + c_row).astype(jnp.float32)
    v_line = v_row.astype(jnp.float32)
    for y in range(TILE):
        away = jnp.abs(line + v_line * float(y)) * (1.0 / TILE)
        wt_ref[y * TILE : (y + 1) * TILE, :] = jnp.maximum(1.0 - away, 0.0).astype(jnp.bfloat16)


def back_kernel(tiles_across, tiles_down, scale, step_ref, other_ref, own_ref, wt_ref, out_ref, g_ref, *scratch):
    chips = other_ref.shape[0]
    win = g_ref.shape[1]
    half = tiles_down // 2
    acc_refs = scratch[-2:]
    step = pl.program_id(0)
    slices = LANES // 2
    angles = slot_angles(0, chips) + slot_angles(1, chips)
    slots = len(angles)

    @pl.when(step == 0)
    def _():
        windows = [other_ref.at[c] for c in range(chips)]
        spread(windows, angles[slots // 2 :], step_ref, tiles_across, tiles_down, win, g_ref, scratch[:4])

    def multiply(acc_ref):
        u = [step_ref[0, a] for a in angles]
        v = [step_ref[1, a] for a in angles]
        base = [v[s] * step - low_corner(u[s], v[s], tiles_across, tiles_down) for s in range(slots)]
        for first in range(0, tiles_across, 2):
            sides = []
            for i in (first, first + 1):
                bands = []
                for s in range(slots):
                    ref, row = (own_ref, s) if s < slots // 2 else (g_ref, s - slots // 2)
                    bands.append(ref[row, pl.ds(base[s] + u[s] * i, BAND), :].astype(jnp.bfloat16))
                sides.append(jnp.concatenate(bands, axis=0))
            bands = jnp.concatenate(sides, axis=1)
            tile = jnp.dot(wt_ref[...], bands, preferred_element_type=jnp.float32)
            tile = (tile * scale).astype(jnp.bfloat16)
            for e in range(2):
                for y in range(TILE):
                    acc_ref[y, (first + e) * TILE : (first + e + 1) * TILE, :] = tile[
                        y * TILE : (y + 1) * TILE, e * LANES : (e + 1) * LANES
                    ]

    def turn(acc_ref):
        for y in range(TILE):
            for part in range(tiles_across * TILE // LANES):
                cols = slice(part * LANES, (part + 1) * LANES)
                turned = acc_ref[y, cols, :].T
                out_ref[0, 0, y, :, cols] = turned[0:slices]
                out_ref[1, 0, y, :, cols] = turned[slices:]

    for parity in range(2):

        @pl.when((step < half) & (lax.rem(step, 2) == parity))
        def _(parity=parity):
            turn(acc_refs[1 - parity])
            multiply(acc_refs[parity])

    @pl.when(step == half)
    def _():
        turn(acc_refs[(half - 1) % 2])


def back_project(own, other, offsets, steps, tiles_across, tiles_down):
    chips = len(own)
    slots = 4 * chips
    win = window_rows(tiles_across, tiles_down)
    half = tiles_down // 2
    cols = tiles_across * TILE
    slices = LANES // 2
    smem = pl.BlockSpec(memory_space=pltpu.SMEM)
    vmem = pl.BlockSpec(memory_space=pltpu.VMEM)
    scale = 2.0 / math.sqrt(slots)
    padded = own[0].shape[0] + 2 * STEP_MAX * half + win
    spread_scratch = [pltpu.VMEM((padded, LANES), jnp.float32)] * 4
    half_spread = jax.ShapeDtypeStruct((slots // 2, win, LANES), jnp.float32)
    params = pltpu.CompilerParams(vmem_limit_bytes=20 * 1024 * 1024)
    own_spread, weights = pl.pallas_call(
        functools.partial(own_kernel, tiles_across, tiles_down, win),
        in_specs=[smem, smem] + [vmem] * chips,
        out_specs=[vmem, vmem],
        out_shape=[half_spread, jax.ShapeDtypeStruct((TILE * TILE, slots * BAND), jnp.bfloat16)],
        scratch_shapes=spread_scratch,
        compiler_params=params,
        cost_estimate=pl.CostEstimate(flops=10**9, bytes_accessed=4 * slots * win * LANES, transcendentals=0),
        name="spread_own",
    )(offsets, steps, *own)
    out = pl.pallas_call(
        functools.partial(back_kernel, tiles_across, tiles_down, scale),
        grid=(half + 1,),
        in_specs=[smem] + [vmem] * 3,
        out_specs=pl.BlockSpec((2, 1, TILE, slices, cols), lambda j: (0, jnp.maximum(j - 1, 0), 0, 0, 0)),
        out_shape=jax.ShapeDtypeStruct((2, half, TILE, slices, cols), jnp.bfloat16),
        scratch_shapes=[pltpu.VMEM(half_spread.shape, jnp.float32)]
        + spread_scratch
        + [pltpu.VMEM((TILE, cols, LANES), jnp.bfloat16)] * 2,
        compiler_params=params,
        cost_estimate=pl.CostEstimate(
            flops=2 * half * cols * TILE * LANES * slots * BAND, bytes_accessed=4 * half * TILE * slices * cols, transcendentals=0
        ),
        name="back_project",
    )(steps, other, own_spread, weights)
    return out.reshape(tiles_down * TILE, slices, cols)


def shards(sinogram, offsets, steps):
    ang_count = lax.axis_size("ang")
    img_count = lax.axis_size("img")
    tiles_across = IMG // img_count // TILE
    tiles_down = IMG // ang_count // TILE
    angles_dev, slices, piece_bins = sinogram.shape
    steps = steps.T
    block = sinogram.reshape(angles_dev * slices, piece_bins)
    chips = ang_count // 2
    windows = filter_windows(block, offsets, steps, img_count, chips, tiles_across, tiles_down)
    own = [windows[0]]
    for slot in range(1, chips):
        own.append(lax.ppermute(windows[slot], "ang", [(i, i ^ (2 * slot)) for i in range(ang_count)]))
    other = lax.ppermute(jnp.stack(own), "ang", [(i, i ^ 1) for i in range(ang_count)])
    return back_project(own, other, offsets, steps, tiles_across, tiles_down)


def solution(mesh):
    return jax.shard_map(
        shards,
        mesh=mesh,
        in_specs=(P("ang", None, "img"), P(), P()),
        out_specs=P("ang", None, "img"),
        check_vma=False,
    )
```

time: 57.4 us -> 55.1 us (0.960)
  the two profiles are of different devices: /device:TPU:17 before, /device:TPU:0 now
where the time goes in v3:
time: 55.1 us; the launch traced here: 54.9 us
  waiting for transfers between devices  23.4 us (42%)
  Pallas kernels  17.4 us (32%)
  starting transfers between devices  11.4 us (21%)
  local copies, waits for them, and re-layouts  2.55 us (5%)
    ppermute x4, waiting for transfers between devices, send(): return lax.ppermute(x, 'img', pairs)  15.6 us
    ppermute x4, starting transfers between devices, send(): return lax.ppermute(x, 'img', pairs)  7.74 us
    pallas_call x1, Pallas kernels, back_project(): pl.pallas_call(functools.partial(back_kernel, tiles_across, tiles_down, s...  7.68 us
    ppermute x3, waiting for transfers between devices, shards(): lax.ppermute(windows[slot], 'ang', [(i, i ^ 2 * slot) for i in range(ang_...  6.86 us
    pallas_call x2, Pallas kernels, partial(): pl.pallas_call(functools.partial(partial_kernel, index, bins, len(seed)),...  4.74 us
    pallas_call x1, Pallas kernels, filter_windows(): pl.pallas_call(functools.partial(late_kernel, plan, targets, tiles_across...  3.63 us
    ppermute x3, starting transfers between devices, shards(): lax.ppermute(windows[slot], 'ang', [(i, i ^ 2 * slot) for i in range(ang_...  3.55 us
    unnamed x10, local copies, waits for them, and re-layouts  2.55 us
  transfers between devices with their start and end apart: 8, of which 5 were waited for; matrix products, arithmetic and copies ran while one was open for 0% of the time, Pallas kernels for 11%

profile of v3, /device:TPU:0, one launch (start us, length us, event | category | flops | bytes accessed | tf_op | source)
XLA Modules:
  0.0 54.9 jit_solution(10598464593442310947)
XLA Ops:
  0.0 3.1 %collective-permute-start.1 = (bf16[128,1024]{1,0:T(8,128)(2,1)}, bf16[128,1024]{1,0:T(8,128)(2,1)S(1)}, u32[]{:S(2)}, u32[]{:S(2)}) collective-permute-start(bf16[128,1024]{1,0:T(8,128)(2,1)} %bitcast.11), channel_id=1, source_target_pairs={{0,1},{1,0},{2,3},{3,2},{4,5},{5,4},{6,7},{7,6},{8,9},{9,8},{10,11... | collective-permute-start | bytes 786440 | tf_op jit(solution)/shard_map/ppermute | solution.py:156
  3.1 2.6 %collective-permute-start = (bf16[128,1024]{1,0:T(8,128)(2,1)}, bf16[128,1024]{1,0:T(8,128)(2,1)S(1)}, u32[]{:S(2)}, u32[]{:S(2)}) collective-permute-start(bf16[128,1024]{1,0:T(8,128)(2,1)} %bitcast.12), channel_id=1, source_target_pairs={{0,2},{1,3},{2,0},{3,1},{4,6},{5,7},{6,4},{7,5},{8,10},{9,11},{10,... | collective-permute-start | bytes 786440 | tf_op jit(solution)/shard_map/ppermute | solution.py:156
  5.6 9.4 %collective-permute-done.1.refs_1_.refs_6_ = bf16[128,1024]{1,0:T(8,128)(2,1)S(1)} collective-permute-done((bf16[128,1024]{1,0:T(8,128)(2,1)}, bf16[128,1024]{1,0:T(8,128)(2,1)S(1)}, u32[]{:S(2)}, u32[]{:S(2)}) %collective-permute-start.1) | collective-permute-done | bytes 262176 | tf_op jit(solution)/shard_map/ppermute | solution.py:156
  15.1 1.6 %copy-done = bf16[8064,128]{1,0:T(8,128)(2,1)S(1)} copy-done((bf16[8064,128]{1,0:T(8,128)(2,1)S(1)}, bf16[8064,128]{1,0:T(8,128)(2,1)}, u32[]{:S(2)}) %copy-start) | copy-done | bytes 2064408
  16.6 0.9 %copy-done.1 = bf16[2,64,1024]{2,1,0:T(8,128)(2,1)S(1)} copy-done((bf16[2,64,1024]{2,1,0:T(8,128)(2,1)S(1)}, bf16[2,64,1024]{2,1,0:T(8,128)(2,1)}, u32[]{:S(2)}) %copy-start.1) | copy-done | bytes 262168
  17.6 2.9 %filter_part2.1.refs_0_ = f32[16,128,256]{2,1,0:T(8,128)S(1)} custom-call(bf16[8064,128]{1,0:T(8,128)(2,1)S(1)} %copy-done, bf16[128,1024]{1,0:T(8,128)(2,1)S(1)} %bitcast.13, bf16[128,1024]{1,0:T(8,128)(2,1)S(1)} %collective-permute-done.1.refs_1_.refs_6_), custom_call_target="tpu_custom_call" | custom-call | flops 2147483648 | bytes 4194304 | tf_op jit(solution)/shard_map/filter_part2/pallas_call | solution.py:143
  20.5 0.0 copy-start.2
  20.5 0.0 copy-start.3
  20.5 0.0 copy-start.4
  20.5 0.8 %collective-permute-start.2 = (bf16[128,1024]{1,0:T(8,128)(2,1)S(1)}, bf16[128,1024]{1,0:T(8,128)(2,1)S(1)}, u32[]{:S(2)}, u32[]{:S(2)}) collective-permute-start(bf16[128,1024]{1,0:T(8,128)(2,1)S(1)} %bitcast.14), channel_id=1, source_target_pairs={{1,2},{2,1},{5,6},{6,5},{9,10},{10,9},{13,14},{14,13},{17,18},{18,... | collective-permute-start | bytes 786440 | tf_op jit(solution)/shard_map/ppermute | solution.py:156
  21.3 1.3 %collective-permute-start.3 = (bf16[128,1024]{1,0:T(8,128)(2,1)S(1)}, bf16[128,1024]{1,0:T(8,128)(2,1)S(1)}, u32[]{:S(2)}, u32[]{:S(2)}) collective-permute-start(bf16[128,1024]{1,0:T(8,128)(2,1)S(1)} %collective-permute-done.refs_1_.refs_7_), channel_id=1, source_target_pairs={{2,3},{1,0},{6,7},{5,4},{10,11},{9,8},{14,15},{13,12},{18,19},{17,... | collective-permute-start | bytes 786440 | tf_op jit(solution)/shard_map/ppermute | solution.py:156
  22.6 1.9 %filter_part1.1.refs_4_ = f32[16,128,256]{2,1,0:T(8,128)S(1)} custom-call(bf16[8064,128]{1,0:T(8,128)(2,1)S(1)} %copy-done, f32[16,128,256]{2,1,0:T(8,128)S(1)} %filter_part2.1.refs_0_, bf16[128,1024]{1,0:T(8,128)(2,1)S(1)} %collective-permute-done.refs_1_.refs_7_), custom_call_target="tpu_custom_call" | custom-call | flops 1073741824 | bytes 4194304 | tf_op jit(solution)/shard_map/filter_part1/pallas_call | solution.py:143
  24.5 6.2 %collective-permute-done.3.refs_9_ = bf16[128,1024]{1,0:T(8,128)(2,1)S(1)} collective-permute-done((bf16[128,1024]{1,0:T(8,128)(2,1)S(1)}, bf16[128,1024]{1,0:T(8,128)(2,1)S(1)}, u32[]{:S(2)}, u32[]{:S(2)}) %collective-permute-start.3) | collective-permute-done | bytes 262176 | tf_op jit(solution)/shard_map/ppermute | solution.py:156
  30.7 3.6 %filter_late.1 = (bf16[736,128]{1,0:T(8,128)(2,1)S(1)}, bf16[736,128]{1,0:T(8,128)(2,1)S(1)}, bf16[736,128]{1,0:T(8,128)(2,1)S(1)}, bf16[736,128]{1,0:T(8,128)(2,1)S(1)}) custom-call(s32[16]{0:T(128)S(1)} %copy-done.3, s32[2,16]{1,0:T(2,128)S(1)} %bitcast.16, bf16[8064,128]{1,0:T(8,128)(2,1)S(1)} %copy-done, bf16[640,128]{1,0:T(8,128)(2,1)S(1)} %copy-done.4, ...), custom_call_target="tpu_custom_call" | custom-call | flops 1610612736 | bytes 4194304 | tf_op jit(solution)/shard_map/filter_late/pallas_call | solution.py:184
  34.4 1.5 %collective-permute-start.4 = (bf16[736,128]{1,0:T(8,128)(2,1)S(1)}, bf16[736,128]{1,0:T(8,128)(2,1)S(1)}, u32[]{:S(2)}, u32[]{:S(2)}) collective-permute-start(bf16[736,128]{1,0:T(8,128)(2,1)S(1)} %get-tuple-element.18), channel_id=1, source_target_pairs={{0,8},{4,12},{8,0},{12,4},{16,24},{20,28},{24,16},{28,20},{1,9},{5... | collective-permute-start | bytes 565256 | tf_op jit(solution)/shard_map/ppermute | solution.py:375
  35.9 1.6 %collective-permute-start.5 = (bf16[736,128]{1,0:T(8,128)(2,1)S(1)}, bf16[736,128]{1,0:T(8,128)(2,1)S(1)}, u32[]{:S(2)}, u32[]{:S(2)}) collective-permute-start(bf16[736,128]{1,0:T(8,128)(2,1)S(1)} %get-tuple-element.19), channel_id=1, source_target_pairs={{0,16},{4,20},{8,24},{12,28},{16,0},{20,4},{24,8},{28,12},{1,17},{... | collective-permute-start | bytes 565256 | tf_op jit(solution)/shard_map/ppermute | solution.py:375
  37.4 0.5 collective-permute-start.6
  37.9 3.7 %collective-permute-done.4.refs_3_ = bf16[736,128]{1,0:T(8,128)(2,1)S(1)} collective-permute-done((bf16[736,128]{1,0:T(8,128)(2,1)S(1)}, bf16[736,128]{1,0:T(8,128)(2,1)S(1)}, u32[]{:S(2)}, u32[]{:S(2)}) %collective-permute-start.4) | collective-permute-done | bytes 188448 | tf_op jit(solution)/shard_map/ppermute | solution.py:375
  41.6 3.2 %collective-permute-done.5.refs_4_ = bf16[736,128]{1,0:T(8,128)(2,1)S(1)} collective-permute-done((bf16[736,128]{1,0:T(8,128)(2,1)S(1)}, bf16[736,128]{1,0:T(8,128)(2,1)S(1)}, u32[]{:S(2)}, u32[]{:S(2)}) %collective-permute-start.5) | collective-permute-done | bytes 188448 | tf_op jit(solution)/shard_map/ppermute | solution.py:375
  44.8 0.1 pad_maximum_fusion
  44.9 0.1 collective-permute-start.7
  44.9 1.3 %spread_own.1 = (f32[8,592,128]{2,1,0:T(8,128)S(1)}, bf16[256,768]{1,0:T(8,128)(2,1)S(1)}) custom-call(s32[16]{0:T(128)S(1)} %copy-done.3, s32[2,16]{1,0:T(2,128)S(1)} %bitcast.17, bf16[736,128]{1,0:T(8,128)(2,1)S(1)} %get-tuple-element.17.refs_2_, bf16[736,128]{1,0:T(8,128)(2,1)S(1)} %collective-permute-done.4.refs_3_, ...), custom_call_target="tpu_custom_call" | custom-call | flops 1000000000 | bytes 4849664 | tf_op jit(solution)/shard_map/spread_own/pallas_call | solution.py:335
  46.3 0.9 %collective-permute-done.7.other_ref = bf16[4,736,128]{2,1,0:T(8,128)(2,1)S(1)} collective-permute-done((bf16[4,736,128]{2,1,0:T(8,128)(2,1)S(1)}, bf16[4,736,128]{2,1,0:T(8,128)(2,1)S(1)}, u32[]{:S(2)}, u32[]{:S(2)}) %collective-permute-start.7) | collective-permute-done | bytes 753696 | tf_op jit(solution)/shard_map/ppermute | solution.py:376
  47.2 7.7 %back_project.1 = bf16[2,4,16,64,256]{4,3,2,1,0:T(8,128)(2,1)} custom-call(s32[2,16]{1,0:T(2,128)S(1)} %bitcast.18, bf16[4,736,128]{2,1,0:T(8,128)(2,1)S(1)} %collective-permute-done.7.other_ref, f32[8,592,128]{2,1,0:T(8,128)S(1)} %get-tuple-element.21.own_ref, bf16[256,768]{1,0:T(8,128)(2,1)S(1)} %get-tuple-element.22.wt_ref), custom_call_target="tpu_custom_call" | custom-call | flops 3221225472 | bytes 4194304 | tf_op jit(solution)/shard_map/back_project/pallas_call | solution.py:345
  (8 shorter events, 0.0 us)
Async XLA Ops:
  0.0 15.1 %collective-permute-start.1 = (bf16[128,1024]{1,0:T(8,128)(2,1)}, bf16[128,1024]{1,0:T(8,128)(2,1)S(1)}, u32[]{:S(2)}, u32[]{:S(2)}) collective-permute-start(bf16[128,1024]{1,0:T(8,128)(2,1)} %bitcast.11), channel_id=1, source_target_pairs={{0,1},{1,0},{2,3},{3,2},{4,5},{5,4},{6,7},{7,6},{8,9},{9,8},{10,11... | collective-permute-start | bytes 786440 | tf_op jit(solution)/shard_map/ppermute | solution.py:156
  3.1 17.5 %collective-permute-start = (bf16[128,1024]{1,0:T(8,128)(2,1)}, bf16[128,1024]{1,0:T(8,128)(2,1)S(1)}, u32[]{:S(2)}, u32[]{:S(2)}) collective-permute-start(bf16[128,1024]{1,0:T(8,128)(2,1)} %bitcast.12), channel_id=1, source_target_pairs={{0,2},{1,3},{2,0},{3,1},{4,6},{5,7},{6,4},{7,5},{8,10},{9,11},{10,... | collective-permute-start | bytes 786440 | tf_op jit(solution)/shard_map/ppermute | solution.py:156
  15.1 1.6 %copy-start = (bf16[8064,128]{1,0:T(8,128)(2,1)S(1)}, bf16[8064,128]{1,0:T(8,128)(2,1)}, u32[]{:S(2)}) copy-start(bf16[8064,128]{1,0:T(8,128)(2,1)} %constant.4.clone.hi_ref.refs_2_) | copy-start | bytes 6193156
  16.6 0.9 %copy-start.1 = (bf16[2,64,1024]{2,1,0:T(8,128)(2,1)S(1)}, bf16[2,64,1024]{2,1,0:T(8,128)(2,1)}, u32[]{:S(2)}) copy-start(bf16[2,64,1024]{2,1,0:T(8,128)(2,1)} %param.5) | copy-start | bytes 786436
  20.5 10.2 %copy-start.2 = (s32[16,2]{0,1:T(2,128)S(1)}, s32[16,2]{0,1:T(2,128)}, u32[]{:S(2)}) copy-start(s32[16,2]{0,1:T(2,128)} %param.7) | copy-start | bytes 388
  20.5 10.2 %copy-start.3 = (s32[16]{0:T(128)S(1)}, s32[16]{0:T(128)}, u32[]{:S(2)}) copy-start(s32[16]{0:T(128)} %refs_0_.3) | copy-start | bytes 196
  20.5 10.2 %copy-start.4 = (bf16[640,128]{1,0:T(8,128)(2,1)S(1)}, bf16[640,128]{1,0:T(8,128)(2,1)}, u32[]{:S(2)}) copy-start(bf16[640,128]{1,0:T(8,128)(2,1)} %constant.5.clone.refs_3_) | copy-start | bytes 491524
  20.5 4.0 %collective-permute-start.2 = (bf16[128,1024]{1,0:T(8,128)(2,1)S(1)}, bf16[128,1024]{1,0:T(8,128)(2,1)S(1)}, u32[]{:S(2)}, u32[]{:S(2)}) collective-permute-start(bf16[128,1024]{1,0:T(8,128)(2,1)S(1)} %bitcast.14), channel_id=1, source_target_pairs={{1,2},{2,1},{5,6},{6,5},{9,10},{10,9},{13,14},{14,13},{17,18},{18,... | collective-permute-start | bytes 786440 | tf_op jit(solution)/shard_map/ppermute | solution.py:156
  21.3 9.4 %collective-permute-start.3 = (bf16[128,1024]{1,0:T(8,128)(2,1)S(1)}, bf16[128,1024]{1,0:T(8,128)(2,1)S(1)}, u32[]{:S(2)}, u32[]{:S(2)}) collective-permute-start(bf16[128,1024]{1,0:T(8,128)(2,1)S(1)} %collective-permute-done.refs_1_.refs_7_), channel_id=1, source_target_pairs={{2,3},{1,0},{6,7},{5,4},{10,11},{9,8},{14,15},{13,12},{18,19},{17,... | collective-permute-start | bytes 786440 | tf_op jit(solution)/shard_map/ppermute | solution.py:156
  34.4 7.2 %collective-permute-start.4 = (bf16[736,128]{1,0:T(8,128)(2,1)S(1)}, bf16[736,128]{1,0:T(8,128)(2,1)S(1)}, u32[]{:S(2)}, u32[]{:S(2)}) collective-permute-start(bf16[736,128]{1,0:T(8,128)(2,1)S(1)} %get-tuple-element.18), channel_id=1, source_target_pairs={{0,8},{4,12},{8,0},{12,4},{16,24},{20,28},{24,16},{28,20},{1,9},{5... | collective-permute-start | bytes 565256 | tf_op jit(solution)/shard_map/ppermute | solution.py:375
  35.9 8.9 %collective-permute-start.5 = (bf16[736,128]{1,0:T(8,128)(2,1)S(1)}, bf16[736,128]{1,0:T(8,128)(2,1)S(1)}, u32[]{:S(2)}, u32[]{:S(2)}) collective-permute-start(bf16[736,128]{1,0:T(8,128)(2,1)S(1)} %get-tuple-element.19), channel_id=1, source_target_pairs={{0,16},{4,20},{8,24},{12,28},{16,0},{20,4},{24,8},{28,12},{1,17},{... | collective-permute-start | bytes 565256 | tf_op jit(solution)/shard_map/ppermute | solution.py:375
  37.4 7.3 %collective-permute-start.6 = (bf16[736,128]{1,0:T(8,128)(2,1)S(1)}, bf16[736,128]{1,0:T(8,128)(2,1)S(1)}, u32[]{:S(2)}, u32[]{:S(2)}) collective-permute-start(bf16[736,128]{1,0:T(8,128)(2,1)S(1)} %get-tuple-element.20), channel_id=1, source_target_pairs={{0,24},{4,28},{8,16},{12,20},{16,8},{20,12},{24,0},{28,4},{1,25},{... | collective-permute-start | bytes 565256 | tf_op jit(solution)/shard_map/ppermute | solution.py:375
  44.9 2.3 %collective-permute-start.7 = (bf16[4,736,128]{2,1,0:T(8,128)(2,1)S(1)}, bf16[4,736,128]{2,1,0:T(8,128)(2,1)S(1)}, u32[]{:S(2)}, u32[]{:S(2)}) collective-permute-start(bf16[4,736,128]{2,1,0:T(8,128)(2,1)S(1)} %pad_maximum_fusion), channel_id=1, source_target_pairs={{0,4},{4,0},{8,12},{12,8},{16,20},{20,16},{24,28},{28,24},{1,5},{5... | collective-permute-start | bytes 2261000 | tf_op jit(solution)/shard_map/ppermute | solution.py:376

commit v4 on v3

--- a/solution.py
+++ b/solution.py
@@ -158,11 +158,11 @@
     if count == 4:
         far = send(block, [(i, i ^ 2) for i in range(4)])
         near = send(block, [(i, i ^ 1) for i in range(4)])
-        part = partial(lambda z: [z, z ^ 1], [block, near])
-        far, again, part = lax.optimization_barrier((far, block, part))
+        part = partial(lambda z: [z], [block])
         ends = send(far, [(2, 3), (1, 0)])
+        again, part = lax.optimization_barrier((block, far, part))[::2]
         middle = send(again, [(1, 2), (2, 1)])
-        part = partial(lambda z: [z ^ 2], [far], part)
+        part = partial(lambda z: [z ^ 1, z ^ 2], [near, far], part)
         pieces = [block, near, far, middle, ends]
 
         def plan(z, refs):

time: 55.1 us -> 53.4 us (0.969)
  the two profiles are of different devices: /device:TPU:0 before, /device:TPU:17 now
where the time goes in v4:
time: 53.4 us; the launch traced here: 53.2 us
  waiting for transfers between devices  17.7 us (33%)
  Pallas kernels  17.4 us (33%)
  starting transfers between devices  15.4 us (29%)
  local copies, waits for them, and re-layouts  2.55 us (5%)
    ppermute x4, starting transfers between devices, send(): return lax.ppermute(x, 'img', pairs)  10.1 us
    ppermute x4, waiting for transfers between devices, send(): return lax.ppermute(x, 'img', pairs)  9.64 us
    pallas_call x1, Pallas kernels, back_project(): pl.pallas_call(functools.partial(back_kernel, tiles_across, tiles_down, s...  7.67 us
    ppermute x3, waiting for transfers between devices, shards(): lax.ppermute(windows[slot], 'ang', [(i, i ^ 2 * slot) for i in range(ang_...  7.49 us
    pallas_call x2, Pallas kernels, partial(): pl.pallas_call(functools.partial(partial_kernel, index, bins, len(seed)),...  4.73 us
    pallas_call x1, Pallas kernels, filter_windows(): pl.pallas_call(functools.partial(late_kernel, plan, targets, tiles_across...  3.71 us
    ppermute x3, starting transfers between devices, shards(): lax.ppermute(windows[slot], 'ang', [(i, i ^ 2 * slot) for i in range(ang_...  2.71 us
    ppermute x1, starting transfers between devices, shards(): lax.ppermute(jnp.stack(own), 'ang', [(i, i ^ 1) for i in range(ang_count)])  2.6 us
  transfers between devices with their start and end apart: 8, of which 7 were waited for; matrix products, arithmetic and copies ran while one was open for 0% of the time, Pallas kernels for 11%

profile of v4, /device:TPU:17, one launch (start us, length us, event | category | flops | bytes accessed | tf_op | source)
XLA Modules:
  0.0 53.2 jit_solution(4208170485765439459)
XLA Ops:
  0.0 1.3 %collective-permute-start.1 = (bf16[128,1024]{1,0:T(8,128)(2,1)}, bf16[128,1024]{1,0:T(8,128)(2,1)S(1)}, u32[]{:S(2)}, u32[]{:S(2)}) collective-permute-start(bf16[128,1024]{1,0:T(8,128)(2,1)} %bitcast.8), channel_id=1, source_target_pairs={{0,1},{1,0},{2,3},{3,2},{4,5},{5,4},{6,7},{7,6},{8,9},{9,8},{10,11... | collective-permute-start | bytes 786440 | tf_op jit(solution)/shard_map/ppermute | solution.py:156
  1.4 1.6 %copy-done = bf16[8064,128]{1,0:T(8,128)(2,1)S(1)} copy-done((bf16[8064,128]{1,0:T(8,128)(2,1)S(1)}, bf16[8064,128]{1,0:T(8,128)(2,1)}, u32[]{:S(2)}) %copy-start) | copy-done | bytes 2064408
  2.9 0.9 %copy-done.1 = bf16[2,64,1024]{2,1,0:T(8,128)(2,1)S(1)} copy-done((bf16[2,64,1024]{2,1,0:T(8,128)(2,1)S(1)}, bf16[2,64,1024]{2,1,0:T(8,128)(2,1)}, u32[]{:S(2)}) %copy-start.1) | copy-done | bytes 262168
  3.9 1.8 %filter_part1.1.refs_0_ = f32[16,128,256]{2,1,0:T(8,128)S(1)} custom-call(bf16[8064,128]{1,0:T(8,128)(2,1)S(1)} %copy-done, bf16[128,1024]{1,0:T(8,128)(2,1)S(1)} %bitcast.9), custom_call_target="tpu_custom_call" | custom-call | flops 1073741824 | bytes 4194304 | tf_op jit(solution)/shard_map/filter_part1/pallas_call | solution.py:143
  5.7 0.0 copy-start.3
  5.7 0.0 copy-start.4
  5.8 5.5 %collective-permute-done.refs_2_.refs_7_ = bf16[128,1024]{1,0:T(8,128)(2,1)S(1)} collective-permute-done((bf16[128,1024]{1,0:T(8,128)(2,1)}, bf16[128,1024]{1,0:T(8,128)(2,1)S(1)}, u32[]{:S(2)}, u32[]{:S(2)}) %collective-permute-start) | collective-permute-done | bytes 262176 | tf_op jit(solution)/shard_map/ppermute | solution.py:156
  11.3 6.8 %collective-permute-start.3 = (bf16[128,1024]{1,0:T(8,128)(2,1)S(1)}, bf16[128,1024]{1,0:T(8,128)(2,1)S(1)}, u32[]{:S(2)}, u32[]{:S(2)}) collective-permute-start(bf16[128,1024]{1,0:T(8,128)(2,1)S(1)} %collective-permute-done.refs_2_.refs_7_), channel_id=1, source_target_pairs={{2,3},{1,0},{6,7},{5,4},{10,11},{9,8},{14,15},{13,12},{18,19},{17,... | collective-permute-start | bytes 786440 | tf_op jit(solution)/shard_map/ppermute | solution.py:156
  18.1 1.9 %collective-permute-start.2 = (bf16[128,1024]{1,0:T(8,128)(2,1)S(1)}, bf16[128,1024]{1,0:T(8,128)(2,1)S(1)}, u32[]{:S(2)}, u32[]{:S(2)}) collective-permute-start(bf16[128,1024]{1,0:T(8,128)(2,1)S(1)} %bitcast.10), channel_id=1, source_target_pairs={{1,2},{2,1},{5,6},{6,5},{9,10},{10,9},{13,14},{14,13},{17,18},{18,... | collective-permute-start | bytes 786440 | tf_op jit(solution)/shard_map/ppermute | solution.py:156
  20.0 2.9 %filter_part2.1.refs_4_ = f32[16,128,256]{2,1,0:T(8,128)S(1)} custom-call(bf16[8064,128]{1,0:T(8,128)(2,1)S(1)} %copy-done, f32[16,128,256]{2,1,0:T(8,128)S(1)} %filter_part1.1.refs_0_, bf16[128,1024]{1,0:T(8,128)(2,1)S(1)} %collective-permute-done.1.refs_1_.refs_6_, bf16[128,1024]{1,0:T(8,128)(2,1)S(1)} %collective-permute-done.refs_2_.refs_7_), custom_call_target="tpu_custom_call" | custom-call | flops 2147483648 | bytes 4194304 | tf_op jit(solution)/shard_map/filter_part2/pallas_call | solution.py:143
  22.9 0.3 collective-permute-done.3.refs_9_
  23.2 3.8 %collective-permute-done.2.refs_8_ = bf16[128,1024]{1,0:T(8,128)(2,1)S(1)} collective-permute-done((bf16[128,1024]{1,0:T(8,128)(2,1)S(1)}, bf16[128,1024]{1,0:T(8,128)(2,1)S(1)}, u32[]{:S(2)}, u32[]{:S(2)}) %collective-permute-start.2) | collective-permute-done | bytes 262176 | tf_op jit(solution)/shard_map/ppermute | solution.py:156
  27.1 3.7 %filter_late.1 = (bf16[736,128]{1,0:T(8,128)(2,1)S(1)}, bf16[736,128]{1,0:T(8,128)(2,1)S(1)}, bf16[736,128]{1,0:T(8,128)(2,1)S(1)}, bf16[736,128]{1,0:T(8,128)(2,1)S(1)}) custom-call(s32[16]{0:T(128)S(1)} %copy-done.3, s32[2,16]{1,0:T(2,128)S(1)} %bitcast.16, bf16[8064,128]{1,0:T(8,128)(2,1)S(1)} %copy-done, bf16[640,128]{1,0:T(8,128)(2,1)S(1)} %copy-done.4, ...), custom_call_target="tpu_custom_call" | custom-call | flops 1610612736 | bytes 4194304 | tf_op jit(solution)/shard_map/filter_late/pallas_call | solution.py:184
  30.8 1.3 %collective-permute-start.4 = (bf16[736,128]{1,0:T(8,128)(2,1)S(1)}, bf16[736,128]{1,0:T(8,128)(2,1)S(1)}, u32[]{:S(2)}, u32[]{:S(2)}) collective-permute-start(bf16[736,128]{1,0:T(8,128)(2,1)S(1)} %get-tuple-element.16), channel_id=1, source_target_pairs={{0,8},{4,12},{8,0},{12,4},{16,24},{20,28},{24,16},{28,20},{1,9},{5... | collective-permute-start | bytes 565256 | tf_op jit(solution)/shard_map/ppermute | solution.py:375
  32.0 1.3 %collective-permute-start.5 = (bf16[736,128]{1,0:T(8,128)(2,1)S(1)}, bf16[736,128]{1,0:T(8,128)(2,1)S(1)}, u32[]{:S(2)}, u32[]{:S(2)}) collective-permute-start(bf16[736,128]{1,0:T(8,128)(2,1)S(1)} %get-tuple-element.17), channel_id=1, source_target_pairs={{0,16},{4,20},{8,24},{12,28},{16,0},{20,4},{24,8},{28,12},{1,17},{... | collective-permute-start | bytes 565256 | tf_op jit(solution)/shard_map/ppermute | solution.py:375
  33.3 0.2 collective-permute-start.6
  33.5 1.8 %collective-permute-done.4.refs_3_ = bf16[736,128]{1,0:T(8,128)(2,1)S(1)} collective-permute-done((bf16[736,128]{1,0:T(8,128)(2,1)S(1)}, bf16[736,128]{1,0:T(8,128)(2,1)S(1)}, u32[]{:S(2)}, u32[]{:S(2)}) %collective-permute-start.4) | collective-permute-done | bytes 188448 | tf_op jit(solution)/shard_map/ppermute | solution.py:375
  35.3 1.7 %collective-permute-done.5.refs_4_ = bf16[736,128]{1,0:T(8,128)(2,1)S(1)} collective-permute-done((bf16[736,128]{1,0:T(8,128)(2,1)S(1)}, bf16[736,128]{1,0:T(8,128)(2,1)S(1)}, u32[]{:S(2)}, u32[]{:S(2)}) %collective-permute-start.5) | collective-permute-done | bytes 188448 | tf_op jit(solution)/shard_map/ppermute | solution.py:375
  37.0 4.0 %collective-permute-done.6.refs_5_ = bf16[736,128]{1,0:T(8,128)(2,1)S(1)} collective-permute-done((bf16[736,128]{1,0:T(8,128)(2,1)S(1)}, bf16[736,128]{1,0:T(8,128)(2,1)S(1)}, u32[]{:S(2)}, u32[]{:S(2)}) %collective-permute-start.6) | collective-permute-done | bytes 188448 | tf_op jit(solution)/shard_map/ppermute | solution.py:375
  41.0 0.1 pad_maximum_fusion
  41.1 2.6 %collective-permute-start.7 = (bf16[4,736,128]{2,1,0:T(8,128)(2,1)S(1)}, bf16[4,736,128]{2,1,0:T(8,128)(2,1)S(1)}, u32[]{:S(2)}, u32[]{:S(2)}) collective-permute-start(bf16[4,736,128]{2,1,0:T(8,128)(2,1)S(1)} %pad_maximum_fusion), channel_id=1, source_target_pairs={{0,4},{4,0},{8,12},{12,8},{16,20},{20,16},{24,28},{28,24},{1,5},{5... | collective-permute-start | bytes 2261000 | tf_op jit(solution)/shard_map/ppermute | solution.py:376
  43.7 1.3 %spread_own.1 = (f32[8,592,128]{2,1,0:T(8,128)S(1)}, bf16[256,768]{1,0:T(8,128)(2,1)S(1)}) custom-call(s32[16]{0:T(128)S(1)} %copy-done.3, s32[2,16]{1,0:T(2,128)S(1)} %bitcast.17, bf16[736,128]{1,0:T(8,128)(2,1)S(1)} %get-tuple-element.15.refs_2_, bf16[736,128]{1,0:T(8,128)(2,1)S(1)} %collective-permute-done.4.refs_3_, ...), custom_call_target="tpu_custom_call" | custom-call | flops 1000000000 | bytes 4849664 | tf_op jit(solution)/shard_map/spread_own/pallas_call | solution.py:335
  45.0 0.5 collective-permute-done.7.other_ref
  45.5 7.7 %back_project.1 = bf16[2,4,16,64,256]{4,3,2,1,0:T(8,128)(2,1)} custom-call(s32[2,16]{1,0:T(2,128)S(1)} %bitcast.18, bf16[4,736,128]{2,1,0:T(8,128)(2,1)S(1)} %collective-permute-done.7.other_ref, f32[8,592,128]{2,1,0:T(8,128)S(1)} %get-tuple-element.19.own_ref, bf16[256,768]{1,0:T(8,128)(2,1)S(1)} %get-tuple-element.20.wt_ref), custom_call_target="tpu_custom_call" | custom-call | flops 3221225472 | bytes 4194304 | tf_op jit(solution)/shard_map/back_project/pallas_call | solution.py:345
  (8 shorter events, 0.0 us)
Async XLA Ops:
  0.0 11.3 %collective-permute-start = (bf16[128,1024]{1,0:T(8,128)(2,1)}, bf16[128,1024]{1,0:T(8,128)(2,1)S(1)}, u32[]{:S(2)}, u32[]{:S(2)}) collective-permute-start(bf16[128,1024]{1,0:T(8,128)(2,1)} %bitcast.7), channel_id=1, source_target_pairs={{0,2},{1,3},{2,0},{3,1},{4,6},{5,7},{6,4},{7,5},{8,10},{9,11},{10,... | collective-permute-start | bytes 786440 | tf_op jit(solution)/shard_map/ppermute | solution.py:156
  0.0 20.0 %collective-permute-start.1 = (bf16[128,1024]{1,0:T(8,128)(2,1)}, bf16[128,1024]{1,0:T(8,128)(2,1)S(1)}, u32[]{:S(2)}, u32[]{:S(2)}) collective-permute-start(bf16[128,1024]{1,0:T(8,128)(2,1)} %bitcast.8), channel_id=1, source_target_pairs={{0,1},{1,0},{2,3},{3,2},{4,5},{5,4},{6,7},{7,6},{8,9},{9,8},{10,11... | collective-permute-start | bytes 786440 | tf_op jit(solution)/shard_map/ppermute | solution.py:156
  1.4 1.6 %copy-start = (bf16[8064,128]{1,0:T(8,128)(2,1)S(1)}, bf16[8064,128]{1,0:T(8,128)(2,1)}, u32[]{:S(2)}) copy-start(bf16[8064,128]{1,0:T(8,128)(2,1)} %constant.4.clone.hi_ref.refs_2_) | copy-start | bytes 6193156
  2.9 0.9 %copy-start.1 = (bf16[2,64,1024]{2,1,0:T(8,128)(2,1)S(1)}, bf16[2,64,1024]{2,1,0:T(8,128)(2,1)}, u32[]{:S(2)}) copy-start(bf16[2,64,1024]{2,1,0:T(8,128)(2,1)} %param.5) | copy-start | bytes 786436
  5.7 21.3 %copy-start.2 = (s32[16,2]{0,1:T(2,128)S(1)}, s32[16,2]{0,1:T(2,128)}, u32[]{:S(2)}) copy-start(s32[16,2]{0,1:T(2,128)} %param.7) | copy-start | bytes 388
  5.7 21.3 %copy-start.3 = (s32[16]{0:T(128)S(1)}, s32[16]{0:T(128)}, u32[]{:S(2)}) copy-start(s32[16]{0:T(128)} %refs_0_.3) | copy-start | bytes 196
  5.7 21.3 %copy-start.4 = (bf16[640,128]{1,0:T(8,128)(2,1)S(1)}, bf16[640,128]{1,0:T(8,128)(2,1)}, u32[]{:S(2)}) copy-start(bf16[640,128]{1,0:T(8,128)(2,1)} %constant.5.clone.refs_3_) | copy-start | bytes 491524
  11.3 11.9 %collective-permute-start.3 = (bf16[128,1024]{1,0:T(8,128)(2,1)S(1)}, bf16[128,1024]{1,0:T(8,128)(2,1)S(1)}, u32[]{:S(2)}, u32[]{:S(2)}) collective-permute-start(bf16[128,1024]{1,0:T(8,128)(2,1)S(1)} %collective-permute-done.refs_2_.refs_7_), channel_id=1, source_target_pairs={{2,3},{1,0},{6,7},{5,4},{10,11},{9,8},{14,15},{13,12},{18,19},{17,... | collective-permute-start | bytes 786440 | tf_op jit(solution)/shard_map/ppermute | solution.py:156
  18.1 9.0 %collective-permute-start.2 = (bf16[128,1024]{1,0:T(8,128)(2,1)S(1)}, bf16[128,1024]{1,0:T(8,128)(2,1)S(1)}, u32[]{:S(2)}, u32[]{:S(2)}) collective-permute-start(bf16[128,1024]{1,0:T(8,128)(2,1)S(1)} %bitcast.10), channel_id=1, source_target_pairs={{1,2},{2,1},{5,6},{6,5},{9,10},{10,9},{13,14},{14,13},{17,18},{18,... | collective-permute-start | bytes 786440 | tf_op jit(solution)/shard_map/ppermute | solution.py:156
  30.8 4.5 %collective-permute-start.4 = (bf16[736,128]{1,0:T(8,128)(2,1)S(1)}, bf16[736,128]{1,0:T(8,128)(2,1)S(1)}, u32[]{:S(2)}, u32[]{:S(2)}) collective-permute-start(bf16[736,128]{1,0:T(8,128)(2,1)S(1)} %get-tuple-element.16), channel_id=1, source_target_pairs={{0,8},{4,12},{8,0},{12,4},{16,24},{20,28},{24,16},{28,20},{1,9},{5... | collective-permute-start | bytes 565256 | tf_op jit(solution)/shard_map/ppermute | solution.py:375
  32.0 4.9 %collective-permute-start.5 = (bf16[736,128]{1,0:T(8,128)(2,1)S(1)}, bf16[736,128]{1,0:T(8,128)(2,1)S(1)}, u32[]{:S(2)}, u32[]{:S(2)}) collective-permute-start(bf16[736,128]{1,0:T(8,128)(2,1)S(1)} %get-tuple-element.17), channel_id=1, source_target_pairs={{0,16},{4,20},{8,24},{12,28},{16,0},{20,4},{24,8},{28,12},{1,17},{... | collective-permute-start | bytes 565256 | tf_op jit(solution)/shard_map/ppermute | solution.py:375
  33.3 7.6 %collective-permute-start.6 = (bf16[736,128]{1,0:T(8,128)(2,1)S(1)}, bf16[736,128]{1,0:T(8,128)(2,1)S(1)}, u32[]{:S(2)}, u32[]{:S(2)}) collective-permute-start(bf16[736,128]{1,0:T(8,128)(2,1)S(1)} %get-tuple-element.18), channel_id=1, source_target_pairs={{0,24},{4,28},{8,16},{12,20},{16,8},{20,12},{24,0},{28,4},{1,25},{... | collective-permute-start | bytes 565256 | tf_op jit(solution)/shard_map/ppermute | solution.py:375
  41.1 4.5 %collective-permute-start.7 = (bf16[4,736,128]{2,1,0:T(8,128)(2,1)S(1)}, bf16[4,736,128]{2,1,0:T(8,128)(2,1)S(1)}, u32[]{:S(2)}, u32[]{:S(2)}) collective-permute-start(bf16[4,736,128]{2,1,0:T(8,128)(2,1)S(1)} %pad_maximum_fusion), channel_id=1, source_target_pairs={{0,4},{4,0},{8,12},{12,8},{16,20},{20,16},{24,28},{28,24},{1,5},{5... | collective-permute-start | bytes 2261000 | tf_op jit(solution)/shard_map/ppermute | solution.py:376
